TPU v7x, 32 devices: a whole 2x2x4 slice. The times are simulated.
32 devices in a mesh: dp: 4 (over x, core), fsdp: 8 (over z, y).
Axes of the slice: x: 2, y: 2, z: 4, core: 2. Of those that a mesh axis runs over, the one named last changes fastest.
Arguments:
- inputs: bfloat16 [2, 4, 16, 192, 768], P(None, 'dp', 'fsdp'), may hold values from -6 to 6
- space_in: bfloat16 [768, 2304], P('fsdp'), may hold values from -0.21875 to 0.21875
- space_out: bfloat16 [768, 768], P('fsdp'), may hold values from -1.5 to 1.5
- time_in: bfloat16 [768, 2304], P('fsdp'), may hold values from -0.21875 to 0.21875
- time_out: bfloat16 [768, 768], P('fsdp'), may hold values from -0.4375 to 0.4375
- hidden_in: bfloat16 [768, 3072], P('fsdp'), may hold values from -0.21875 to 0.21875
- hidden_out: bfloat16 [3072, 768], P('fsdp'), may hold values from -0.109375 to 0.109375
- norm_gains: bfloat16 [3, 768], P(None, 'fsdp'), may hold values from 0.5 to 1.5
- cotangent: bfloat16 [2, 4, 16, 192, 768], P(None, 'dp', 'fsdp'), may hold values from -6 to 6
Outputs:
- result: float32 [2, 4, 16, 192, 768], P(None, 'dp', 'fsdp')
- input_grad: float32 [2, 4, 16, 192, 768], P(None, 'dp', 'fsdp')
- grad_space_in: float32 [768, 2304], P('fsdp')
- grad_space_out: float32 [768, 768], P('fsdp')
- grad_time_in: float32 [768, 2304], P('fsdp')
- grad_time_out: float32 [768, 768], P('fsdp')
- grad_hidden_in: float32 [768, 3072], P('fsdp')
- grad_hidden_out: float32 [3072, 768], P('fsdp')
- grad_norm_gains: float32 [3, 768], P(None, 'fsdp')
All inputs are finite; a program needn't handle non-finite values.
Results may differ from a plain program's by a relative error of at most 0.025.
Values may be sent and summed in bfloat16 or wider, within the bound.
A program may use at most 192 MiB of HBM per device.

v0:
```python
from functools import partial

import jax
import jax.numpy as jnp
from jax import lax
from jax.sharding import PartitionSpec as P

D = 768
HEADS = 12
HEAD_DIM = 64


EPS = 1e-06


def as_sent(shard):

    def short(part):
        return part.astype(jnp.bfloat16) if part.dtype == jnp.float32 else part

    return jax.tree.map(short, shard)


def layer_norm(values, scales):
    average = jnp.mean(values, axis=-1, keepdims=True)
    centred = values - average
    spread = jnp.mean(centred * centred, axis=-1, keepdims=True)
    return centred * lax.rsqrt(spread + EPS) * scales


def norm_back(values, scales, incoming):
    unused, pullback = jax.vjp(layer_norm, values, scales)
    return pullback(incoming)


def flat_dot(left, right):
    flat = left.reshape(-1, left.shape[-1])
    product = jnp.dot(flat, right, preferred_element_type=jnp.float32)
    return product.reshape(left.shape[:-1] + (right.shape[1],))


def back_dot(left, right):
    flat = left.reshape(-1, left.shape[-1])
    product = lax.dot_general(
        flat, right, (((1,), (1,)), ((), ())), preferred_element_type=jnp.float32
    )
    return product.reshape(left.shape[:-1] + (right.shape[0],))


def token_sum(left, right):
    left_rows = left.reshape(-1, left.shape[-1])
    right_rows = right.reshape(-1, right.shape[-1])
    return lax.dot_general(
        left_rows, right_rows, (((0,), (0,)), ((), ())), preferred_element_type=jnp.float32
    )


def split_join(joined):
    split_heads = joined.reshape(joined.shape[:2] + (3, HEADS, HEAD_DIM))
    return (split_heads[:, :, 0], split_heads[:, :, 1], split_heads[:, :, 2])


def attend_core(normed, weight_in, token_form, key_form):
    joined = flat_dot(normed, weight_in).astype(jnp.bfloat16)
    queries, keyset, valueset = split_join(joined)
    factor = HEAD_DIM ** (-0.5)
    scores = (
        jnp.einsum(
            token_form + "hd," + key_form + "hd->ghlm",
            queries,
            keyset,
            preferred_element_type=jnp.float32,
        )
        * factor
    )
    totals = jax.nn.logsumexp(scores, axis=-1, keepdims=True)
    weighting = jnp.exp(scores - totals).astype(jnp.bfloat16)
    context = jnp.einsum(
        "ghlm," + key_form + "hd->" + token_form + "hd",
        weighting,
        valueset,
        preferred_element_type=jnp.float32,
    )
    context = context.reshape(normed.shape[:2] + (D,)).astype(jnp.bfloat16)
    return (joined, totals, context)


def attend_back(joined, totals, back_context, token_form, key_form):
    queries, keyset, valueset = split_join(joined)
    back_heads = back_context.reshape(back_context.shape[:2] + (HEADS, HEAD_DIM))
    factor = HEAD_DIM ** (-0.5)
    scores = (
        jnp.einsum(
            token_form + "hd," + key_form + "hd->ghlm",
            queries,
            keyset,
            preferred_element_type=jnp.float32,
        )
        * factor
    )
    weighting = jnp.exp(scores - totals)
    back_weight = jnp.einsum(
        token_form + "hd," + key_form + "hd->ghlm",
        back_heads,
        valueset,
        preferred_element_type=jnp.float32,
    )
    back_weight = back_weight.astype(jnp.bfloat16).astype(jnp.float32)
    inner_sum = jnp.sum(weighting * back_weight, axis=-1, keepdims=True)
    back_scores = (weighting * (back_weight - inner_sum)).astype(jnp.bfloat16)
    back_query = (
        jnp.einsum(
            "ghlm," + key_form + "hd->" + token_form + "hd",
            back_scores,
            keyset,
            preferred_element_type=jnp.float32,
        )
        * factor
    )
    back_keys = (
        jnp.einsum(
            "ghlm," + token_form + "hd->" + key_form + "hd",
            back_scores,
            queries,
            preferred_element_type=jnp.float32,
        )
        * factor
    )
    back_values = jnp.einsum(
        "ghlm," + token_form + "hd->" + key_form + "hd",
        weighting.astype(jnp.bfloat16),
        back_heads,
        preferred_element_type=jnp.float32,
    )
    stacked = jnp.stack((back_query, back_keys, back_values), axis=2)
    return stacked.reshape(back_context.shape[:2] + (3 * D,)).astype(jnp.bfloat16)


def shards(
    inputs, space_in, space_out, time_in, time_out, hidden_in, hidden_out, norm_gains, cotangent
):
    batch_count = inputs.shape[0]
    outputs = []
    input_grads = []
    grad_total = None
    for batch_index in range(batch_count):
        gathered = (
            lax.all_gather(space_in, "fsdp", axis=0, tiled=True),
            lax.all_gather(space_out, "fsdp", axis=0, tiled=True),
            lax.all_gather(time_in, "fsdp", axis=0, tiled=True),
            lax.all_gather(time_out, "fsdp", axis=0, tiled=True),
            lax.all_gather(hidden_in, "fsdp", axis=0, tiled=True),
            lax.all_gather(hidden_out, "fsdp", axis=0, tiled=True),
            lax.all_gather(norm_gains, "fsdp", axis=1, tiled=True),
        )
        gain_rows = gathered[6].astype(jnp.float32)
        frames_in = inputs[batch_index, 0].astype(jnp.float32)
        normed_one = layer_norm(frames_in, gain_rows[0]).astype(jnp.bfloat16)
        join_space, total_space, context_space = attend_core(normed_one, gathered[0], "gl", "gm")
        mixed_one = frames_in + flat_dot(context_space, gathered[1])
        normed_two = layer_norm(mixed_one, gain_rows[1]).astype(jnp.bfloat16)
        placed = lax.all_to_all(normed_two, "fsdp", split_axis=1, concat_axis=0, tiled=True)
        join_time, total_time, context_placed = attend_core(placed, gathered[2], "lg", "mg")
        context_time = lax.all_to_all(
            context_placed, "fsdp", split_axis=0, concat_axis=1, tiled=True
        )
        mixed_two = mixed_one + flat_dot(context_time, gathered[3])
        normed_three = layer_norm(mixed_two, gain_rows[2]).astype(jnp.bfloat16)
        hidden = flat_dot(normed_three, gathered[4])
        activated = jax.nn.gelu(hidden, approximate=False).astype(jnp.bfloat16)
        outputs.append(mixed_two + flat_dot(activated, gathered[5]))
        weights_back = (
            lax.all_gather(space_in, "fsdp", axis=0, tiled=True),
            lax.all_gather(space_out, "fsdp", axis=0, tiled=True),
            lax.all_gather(time_in, "fsdp", axis=0, tiled=True),
            lax.all_gather(time_out, "fsdp", axis=0, tiled=True),
            lax.all_gather(hidden_in, "fsdp", axis=0, tiled=True),
            lax.all_gather(hidden_out, "fsdp", axis=0, tiled=True),
            lax.all_gather(norm_gains, "fsdp", axis=1, tiled=True),
        )
        gain_back = weights_back[6].astype(jnp.float32)
        upstream = cotangent[batch_index, 0].astype(jnp.float32)
        rounded = upstream.astype(jnp.bfloat16)
        grad_hidden_out = token_sum(activated, rounded)
        back_active = back_dot(rounded, weights_back[5]).astype(jnp.bfloat16)
        unused, gelu_pull = jax.vjp(partial(jax.nn.gelu, approximate=False), hidden)
        back_hidden = gelu_pull(back_active.astype(jnp.float32))[0].astype(jnp.bfloat16)
        grad_hidden_in = token_sum(normed_three, back_hidden)
        back_three = back_dot(back_hidden, weights_back[4]).astype(jnp.bfloat16)
        back_mixed, gain_grad_two = norm_back(
            mixed_two, gain_back[2], back_three.astype(jnp.float32)
        )
        upstream = upstream + back_mixed
        rounded = upstream.astype(jnp.bfloat16)
        grad_time_out = token_sum(context_time, rounded)
        back_context = back_dot(rounded, weights_back[3]).astype(jnp.bfloat16)
        back_placed = lax.all_to_all(back_context, "fsdp", split_axis=1, concat_axis=0, tiled=True)
        back_join = attend_back(join_time, total_time, back_placed, "lg", "mg")
        grad_time_in = token_sum(placed, back_join)
        back_two_placed = back_dot(back_join, weights_back[2]).astype(jnp.bfloat16)
        back_two = lax.all_to_all(back_two_placed, "fsdp", split_axis=0, concat_axis=1, tiled=True)
        back_mixed, gain_grad_one = norm_back(mixed_one, gain_back[1], back_two.astype(jnp.float32))
        upstream = upstream + back_mixed
        rounded = upstream.astype(jnp.bfloat16)
        grad_space_out = token_sum(context_space, rounded)
        back_context = back_dot(rounded, weights_back[1]).astype(jnp.bfloat16)
        back_join = attend_back(join_space, total_space, back_context, "gl", "gm")
        grad_space_in = token_sum(normed_one, back_join)
        back_one = back_dot(back_join, weights_back[0]).astype(jnp.bfloat16)
        back_mixed, gain_grad_zero = norm_back(
            frames_in, gain_back[0], back_one.astype(jnp.float32)
        )
        input_grads.append(upstream + back_mixed)
        grad_terms = (
            grad_space_in,
            grad_space_out,
            grad_time_in,
            grad_time_out,
            grad_hidden_in,
            grad_hidden_out,
            jnp.stack((gain_grad_zero, gain_grad_one, gain_grad_two)),
        )
        if grad_total is None:
            grad_total = grad_terms
        else:
            grad_total = jax.tree.map(lambda older, newer: older + newer, grad_total, grad_terms)
    grad_owned = (
        lax.psum_scatter(
            grad_total[0].astype(jnp.bfloat16), "fsdp", scatter_dimension=0, tiled=True
        ).astype(jnp.float32),
        lax.psum_scatter(
            grad_total[1].astype(jnp.bfloat16), "fsdp", scatter_dimension=0, tiled=True
        ).astype(jnp.float32),
        lax.psum_scatter(
            grad_total[2].astype(jnp.bfloat16), "fsdp", scatter_dimension=0, tiled=True
        ).astype(jnp.float32),
        lax.psum_scatter(
            grad_total[3].astype(jnp.bfloat16), "fsdp", scatter_dimension=0, tiled=True
        ).astype(jnp.float32),
        lax.psum_scatter(
            grad_total[4].astype(jnp.bfloat16), "fsdp", scatter_dimension=0, tiled=True
        ).astype(jnp.float32),
        lax.psum_scatter(
            grad_total[5].astype(jnp.bfloat16), "fsdp", scatter_dimension=0, tiled=True
        ).astype(jnp.float32),
        lax.psum_scatter(
            grad_total[6].astype(jnp.bfloat16), "fsdp", scatter_dimension=1, tiled=True
        ).astype(jnp.float32),
    )
    grad_owned = jax.tree.map(
        lambda part: part.astype(jnp.float32), lax.psum(as_sent(grad_owned), "dp")
    )
    result = jnp.stack(outputs)[:, None]
    input_grad = jnp.stack(input_grads)[:, None]
    return (
        result,
        input_grad,
        grad_owned[0],
        grad_owned[1],
        grad_owned[2],
        grad_owned[3],
        grad_owned[4],
        grad_owned[5],
        grad_owned[6],
    )


def solution(mesh):
    placed = (
        P(None, "dp", "fsdp", None, None),
        P("fsdp", None),
        P("fsdp", None),
        P("fsdp", None),
        P("fsdp", None),
        P("fsdp", None),
        P("fsdp", None),
        P(None, "fsdp"),
        P(None, "dp", "fsdp", None, None),
    )
    return jax.shard_map(
        shards,
        mesh=mesh,
        in_specs=placed,
        out_specs=(
            P(None, "dp", "fsdp", None, None),
            P(None, "dp", "fsdp", None, None),
            P("fsdp", None),
            P("fsdp", None),
            P("fsdp", None),
            P("fsdp", None),
            P("fsdp", None),
            P("fsdp", None),
            P(None, "fsdp"),
        ),
        check_vma=False,
    )
```

profile of v0, /device:TPU:0, one launch (start us, length us, event | category | flops | bytes accessed | tf_op | source)
XLA Modules:
  0.0 1206.3 jit_solution(5438285885318143471)
XLA Ops:
  10.6 22.9 %all-gather = bf16[8,96,3]{1,2,0:T(4,128)(2,1)S(1)} all-gather(bf16[1,96,3]{1,2,0:T(4,128)(2,1)} %bitcast.521), channel_id=1, replica_groups=mesh['dp'=4,'fsdp'=8] {'fsdp'}, dimensions={0}, use_global_device_ids=true | all-gather | bytes 5184 | tf_op jit(solution)/shard_map/all_gather | solution.py:154
  35.6 42.0 %all-gather.8.cloned.1.call-done = bf16[768,2304]{1,0:T(8,128)(2,1)} async-done(((bf16[96,2304]{1,0:T(8,128)(2,1)}), bf16[768,2304]{1,0:T(8,128)(2,1)}) %all-gather.8.cloned.1.call-update) | async-done | bytes 3538960 | tf_op jit(solution)/shard_map/all_gather | solution.py:148
  100.6 19.0 %all-gather.10.cloned.1.call-done = bf16[768,768]{1,0:T(8,128)(2,1)} async-done(((bf16[96,768]{1,0:T(8,128)(2,1)}), bf16[768,768]{1,0:T(8,128)(2,1)}) %all-gather.10.cloned.1.call-update) | async-done | bytes 1179664 | tf_op jit(solution)/shard_map/all_gather | solution.py:149
  136.0 23.4 %all-to-all-done.2 = bf16[2,192,768]{2,0,1:T(2,128)(2,1)S(1)} async-done(((bf16[2,192,768]{2,0,1:T(2,128)(2,1)}), bf16[2,192,768]{2,0,1:T(2,128)(2,1)S(1)}, u32[]{:S(2)}, u32[]{:S(2)}) %all-to-all-start.2) | async-done | bytes 589856 | tf_op jit(solution)/shard_map/all_to_all | solution.py:162
  163.3 44.0 %all-gather.12.cloned.1.call-done = bf16[768,2304]{1,0:T(8,128)(2,1)} async-done(((bf16[96,2304]{1,0:T(8,128)(2,1)}), bf16[768,2304]{1,0:T(8,128)(2,1)}) %all-gather.12.cloned.1.call-update) | async-done | bytes 3538960 | tf_op jit(solution)/shard_map/all_gather | solution.py:150
  264.4 25.0 %all-to-all-done.1 = bf16[16,24,768]{2,1,0:T(8,128)(2,1)} async-done(((bf16[16,24,768]{2,1,0:T(8,128)(2,1)}), bf16[16,24,768]{2,1,0:T(8,128)(2,1)}, u32[]{:S(2)}, u32[]{:S(2)}) %all-to-all-start.1) | async-done | bytes 589856 | tf_op jit(solution)/shard_map/all_to_all | solution.py:164
  297.3 48.0 %all-gather.16.cloned.1.call-done = bf16[768,3072]{1,0:T(8,128)(2,1)} async-done(((bf16[96,3072]{1,0:T(8,128)(2,1)}), bf16[768,3072]{1,0:T(8,128)(2,1)}) %all-gather.16.cloned.1.call-update) | async-done | bytes 4718608 | tf_op jit(solution)/shard_map/all_gather | solution.py:152
  353.5 11.9 multiply_convert_fusion.1
  365.4 59.7 %all-gather.18.cloned.1.call-done = bf16[3072,768]{1,0:T(8,128)(2,1)} async-done(((bf16[384,768]{1,0:T(8,128)(2,1)}), bf16[3072,768]{1,0:T(8,128)(2,1)}) %all-gather.18.cloned.1.call-update) | async-done | bytes 4718608 | tf_op jit(solution)/shard_map/all_gather | solution.py:153
  425.0 8.2 fusion.7
  444.8 11.5 multiply_convert_fusion
  480.0 11.2 all-to-all-done.6
  515.1 6.6 convert_element_type.462
  551.1 6.6 convert_element_type.435
  573.1 9.5 all-to-all-done.5
  595.8 6.6 convert_element_type.485
  676.8 6.6 fusion.108
  698.1 8.2 reduce-scatter.12.cloned.1.call-done
  706.3 82.1 %reduce-scatter.14.cloned.1.call-done = bf16[96,2304]{1,0:T(8,128)(2,1)} async-done(((bf16[768,2304]{1,0:T(8,128)(2,1)}), bf16[96,2304]{1,0:T(8,128)(2,1)}) %reduce-scatter.14.cloned.1.call-update) | async-done | bytes 442384 | tf_op jit(solution)/shard_map/reduce_scatter | solution.py:234
  788.4 82.5 %reduce-scatter.10.cloned.1.call-done = bf16[96,2304]{1,0:T(8,128)(2,1)} async-done(((bf16[768,2304]{1,0:T(8,128)(2,1)}), bf16[96,2304]{1,0:T(8,128)(2,1)}) %reduce-scatter.10.cloned.1.call-update) | async-done | bytes 442384 | tf_op jit(solution)/shard_map/reduce_scatter | solution.py:228
  871.0 99.0 %reduce-scatter.18.cloned.1.call-done = bf16[96,3072]{1,0:T(8,128)(2,1)} async-done(((bf16[768,3072]{1,0:T(8,128)(2,1)}), bf16[96,3072]{1,0:T(8,128)(2,1)}) %reduce-scatter.18.cloned.1.call-update) | async-done | bytes 589840 | tf_op jit(solution)/shard_map/reduce_scatter | solution.py:240
  969.9 98.8 %reduce-scatter.20.cloned.1.call-done = bf16[384,768]{1,0:T(8,128)(2,1)} async-done(((bf16[3072,768]{1,0:T(8,128)(2,1)}), bf16[384,768]{1,0:T(8,128)(2,1)}) %reduce-scatter.20.cloned.1.call-update) | async-done | bytes 589840 | tf_op jit(solution)/shard_map/reduce_scatter | solution.py:243
  1074.5 59.7 %reduce-scatter.22.cloned.1.call-done = bf16[96,3]{1,0:T(8,128)(2,1)} async-done(((bf16[768,3]{1,0:T(8,128)(2,1)}), bf16[96,3]{1,0:T(8,128)(2,1)}) %reduce-scatter.22.cloned.1.call-update) | async-done | bytes 592
  1141.2 50.4 %all-reduce.3.cloned.1.call-done = (bf16[96,2304]{1,0:T(8,128)(2,1)}, bf16[96,768]{1,0:T(8,128)(2,1)}, bf16[96,2304]{1,0:T(8,128)(2,1)}, bf16[96,768]{1,0:T(8,12...) async-done(((bf16[96,2304]{1,0:T(8,128)(2,1)}, bf16[96,768]{1,0:T(8,128)(2,1)}, bf16[96,2304]{1,0:T(8,128)(2,1)}, bf16[96,768]{1,0:T(8,128)(2,1)}, ...) | async-done | bytes 2359312 | tf_op jit(solution)/shard_map/psum | solution.py:251
  (534 shorter events, 346.8 us)
Async XLA Ops:
  7.2 70.4 %all-gather.8.cloned.1.call-start = ((), (), s32[]{:S(2)}) async-start(), calls=%async_computation.15 | async-start | bytes 3981312 | tf_op jit(solution)/shard_map/all_gather | solution.py:148
  7.9 111.7 %all-gather.10.cloned.1.call-start = ((), (), s32[]{:S(2)}) async-start(), calls=%async_computation.16 | async-start | bytes 1327104 | tf_op jit(solution)/shard_map/all_gather | solution.py:149
  8.7 198.7 %all-gather.12.cloned.1.call-start = ((), (), s32[]{:S(2)}) async-start(), calls=%async_computation.17 | async-start | bytes 3981312 | tf_op jit(solution)/shard_map/all_gather | solution.py:150
  9.4 281.9 %all-gather.14.cloned.1.call-start = ((), (), s32[]{:S(2)}) async-start(), calls=%async_computation.18 | async-start | bytes 1327104 | tf_op jit(solution)/shard_map/all_gather | solution.py:151
  10.0 335.3 %all-gather.16.cloned.1.call-start = ((), (), s32[]{:S(2)}) async-start(), calls=%async_computation.19 | async-start | bytes 5308416 | tf_op jit(solution)/shard_map/all_gather | solution.py:152
  130.4 29.0 %all-to-all-start.2 = ((bf16[2,192,768]{2,0,1:T(2,128)(2,1)}), bf16[2,192,768]{2,0,1:T(2,128)(2,1)S(1)}, u32[]{:S(2)}, u32[]{:S(2)}) async-start(bf16[2,192,768]{2,0,1:T(2,128)(2,1)} %copy.330), calls=%async_computation.2 | async-start | bytes 1179648 | tf_op jit(solution)/shard_map/all_to_all | solution.py:162
  133.9 291.1 %all-gather.18.cloned.1.call-start = ((), (), s32[]{:S(2)}) async-start(), calls=%async_computation.20 | async-start | bytes 5308416 | tf_op jit(solution)/shard_map/all_gather | solution.py:153
  159.4 68.5 %all-to-all-start = ((bf16[2,192,768]{2,0,1:T(2,128)(2,1)}), bf16[2,192,768]{2,0,1:T(2,128)(2,1)S(1)}, u32[]{:S(2)}, u32[]{:S(2)}) async-start(bf16[2,192,768]{2,0,1:T(2,128)(2,1)} %copy.315), calls=%async_computation | async-start | bytes 1179648 | tf_op jit(solution)/shard_map/all_to_all | solution.py:162
  227.9 29.9 %all-to-all-start.3 = ((bf16[16,24,768]{2,1,0:T(8,128)(2,1)}), bf16[16,24,768]{2,1,0:T(8,128)(2,1)}, u32[]{:S(2)}, u32[]{:S(2)}) async-start(bf16[16,24,768]{2,1,0:T(8,128)(2,1)} %convert_element_type.420), calls=%async_computation.3 | async-start | bytes 1179648 | tf_op jit(solution)/shard_map/all_to_all | solution.py:164
  257.8 31.6 %all-to-all-start.1 = ((bf16[16,24,768]{2,1,0:T(8,128)(2,1)}), bf16[16,24,768]{2,1,0:T(8,128)(2,1)}, u32[]{:S(2)}, u32[]{:S(2)}) async-start(bf16[16,24,768]{2,1,0:T(8,128)(2,1)} %convert_element_type.404), calls=%async_computation.1 | async-start | bytes 1179648 | tf_op jit(solution)/shard_map/all_to_all | solution.py:164
  472.2 19.0 %all-to-all-start.6 = ((bf16[2,192,768]{2,0,1:T(2,128)(2,1)}), bf16[2,192,768]{2,0,1:T(2,128)(2,1)}, u32[]{:S(2)}, u32[]{:S(2)}) async-start(bf16[2,192,768]{2,0,1:T(2,128)(2,1)} %copy.352), calls=%async_computation.6 | async-start | bytes 1179648 | tf_op jit(solution)/shard_map/all_to_all | solution.py:197
  491.2 35.4 %all-to-all-start.4 = ((bf16[2,192,768]{2,0,1:T(2,128)(2,1)}), bf16[2,192,768]{2,0,1:T(2,128)(2,1)}, u32[]{:S(2)}, u32[]{:S(2)}) async-start(bf16[2,192,768]{2,0,1:T(2,128)(2,1)} %copy.339), calls=%async_computation.4 | async-start | bytes 1179648 | tf_op jit(solution)/shard_map/all_to_all | solution.py:197
  526.6 36.1 %all-to-all-start.7 = ((bf16[16,24,768]{2,1,0:T(8,128)(2,1)}), bf16[16,24,768]{2,1,0:T(8,128)(2,1)}, u32[]{:S(2)}, u32[]{:S(2)}) async-start(bf16[16,24,768]{2,1,0:T(8,128)(2,1)} %fusion.126), calls=%async_computation.7 | async-start | bytes 1179648 | tf_op jit(solution)/shard_map/all_to_all | solution.py:201
  562.7 19.8 %all-to-all-start.5 = ((bf16[16,24,768]{2,1,0:T(8,128)(2,1)}), bf16[16,24,768]{2,1,0:T(8,128)(2,1)}, u32[]{:S(2)}, u32[]{:S(2)}) async-start(bf16[16,24,768]{2,1,0:T(8,128)(2,1)} %fusion.123), calls=%async_computation.5 | async-start | bytes 1179648 | tf_op jit(solution)/shard_map/all_to_all | solution.py:201
  568.9 129.2 %reduce-scatter.16.cloned.1.call-start = ((), (), s32[]{:S(2)}) async-start(), calls=%async_computation.24 | async-start | bytes 1327104 | tf_op jit(solution)/shard_map/reduce_scatter | solution.py:237
  571.7 134.6 %reduce-scatter.12.cloned.1.call-start = ((), (), s32[]{:S(2)}) async-start(), calls=%async_computation.22 | async-start | bytes 1327104 | tf_op jit(solution)/shard_map/reduce_scatter | solution.py:231
  595.8 192.6 %reduce-scatter.14.cloned.1.call-start = ((), (), s32[]{:S(2)}) async-start(), calls=%async_computation.23 | async-start | bytes 3981312 | tf_op jit(solution)/shard_map/reduce_scatter | solution.py:234
  615.6 255.4 %reduce-scatter.10.cloned.1.call-start = ((), (), s32[]{:S(2)}) async-start(), calls=%async_computation.21 | async-start | bytes 3981312 | tf_op jit(solution)/shard_map/reduce_scatter | solution.py:228
  655.5 314.4 %reduce-scatter.18.cloned.1.call-start = ((), (), s32[]{:S(2)}) async-start(), calls=%async_computation.25 | async-start | bytes 5308416 | tf_op jit(solution)/shard_map/reduce_scatter | solution.py:240
  666.0 402.7 %reduce-scatter.20.cloned.1.call-start = ((), (), s32[]{:S(2)}) async-start(), calls=%async_computation.26 | async-start | bytes 5308416 | tf_op jit(solution)/shard_map/reduce_scatter | solution.py:243
  676.1 458.1 %reduce-scatter.22.cloned.1.call-start = ((), (), s32[]{:S(2)}) async-start(), calls=%async_computation.27 | async-start | bytes 221184
  692.4 499.2 %all-reduce.3.cloned.1.call-start = ((), (), s32[]{:S(2)}) async-start(), calls=%async_computation.28 | async-start | bytes 4718592 | tf_op jit(solution)/shard_map/psum | solution.py:251
  698.1 370.7 %copy-start.81 = (f32[1,2,192,768]{3,2,1,0:T(8,128)S(1)}, f32[1,2,192,768]{3,2,1,0:T(8,128)}, u32[]{:S(2)}) copy-start(f32[1,2,192,768]{3,2,1,0:T(8,128)} %fusion.108) | copy-start | bytes 3538948
  698.1 370.7 %copy-start.82 = (f32[1,2,192,768]{3,2,1,0:T(8,128)S(1)}, f32[1,2,192,768]{3,2,1,0:T(8,128)}, u32[]{:S(2)}) copy-start(f32[1,2,192,768]{3,2,1,0:T(8,128)} %fusion.114) | copy-start | bytes 3538948
  (155 other events, 907.6 us)
Sparse Core Ops, SparseCore 0:
  10.2 67.3 all-gather.7
  79.7 39.8 all-gather.9
  121.8 85.4 all-gather.11
  209.4 47.9 all-gather.13
  259.4 85.7 all-gather.15
  347.3 77.6 all-gather.17
  573.1 66.0 reduce-scatter.15
  642.6 63.6 reduce-scatter.11
  709.9 78.4 reduce-scatter.13
  791.9 79.0 reduce-scatter.9
  874.6 95.2 reduce-scatter.17
  973.4 95.2 reduce-scatter.19
  1072.6 61.5 reduce-scatter.21
  1136.8 54.7 all-reduce.2
where the time goes:
time: 1210 us
  waiting for transfers between devices  771 us (64%)
  matrix products  170 us (14%)
  local copies, waits for them, and re-layouts  120 us (10%)
  other arithmetic  61.4 us (5%)
  starting transfers between devices  39.2 us (3%)
  blocking collectives  28.5 us (2%)
  between operations  16.4 us (1%)
    reduce_scatter x1, waiting for transfers between devices, shards(): lax.psum_scatter(grad_total[4].astype(jnp.bfloat16), 'fsdp', scatter_dime...  99 us
    reduce_scatter x1, waiting for transfers between devices, shards(): lax.psum_scatter(grad_total[5].astype(jnp.bfloat16), 'fsdp', scatter_dime...  98.8 us
    reduce_scatter x1, waiting for transfers between devices, shards(): lax.psum_scatter(grad_total[0].astype(jnp.bfloat16), 'fsdp', scatter_dime...  82.5 us
    reduce_scatter x1, waiting for transfers between devices, shards(): lax.psum_scatter(grad_total[2].astype(jnp.bfloat16), 'fsdp', scatter_dime...  82.1 us
    unnamed x15, waiting for transfers between devices  63.4 us
    all_gather x1, waiting for transfers between devices, shards(): lax.all_gather(hidden_out, 'fsdp', axis=0, tiled=True)  59.7 us
    psum x1, waiting for transfers between devices, shards(): lax.psum(as_sent(grad_owned), 'dp')  50.4 us
    dot_general x12, matrix products, flat_dot(): product = jnp.dot(flat, right, preferred_element_type=jnp.float32)  49.3 us
  transfers between devices with their start and end apart: 22, of which 17 were waited for; matrix products, arithmetic and copies ran while one was open for 22% of the time, Pallas kernels for 0%

commit v1 on v0

v1 whole, which is shorter than its diff:
```python
from functools import partial

import jax
import jax.numpy as jnp
from jax import lax
from jax.sharding import Mesh
from jax.sharding import PartitionSpec as P

D = 768
HEADS = 12
HEAD_DIM = 64
GAIN_COLS = 128

EPS = 1e-06

MEMBERS = ("fsdp", "core")


def layer_norm(values, scales):
    average = jnp.mean(values, axis=-1, keepdims=True)
    centred = values - average
    spread = jnp.mean(centred * centred, axis=-1, keepdims=True)
    return centred * lax.rsqrt(spread + EPS) * scales


def norm_back(values, scales, incoming):
    unused, pullback = jax.vjp(layer_norm, values, scales)
    return pullback(incoming)


def flat_dot(left, right):
    flat = left.reshape(-1, left.shape[-1])
    product = jnp.dot(flat, right, preferred_element_type=jnp.float32)
    return product.reshape(left.shape[:-1] + (right.shape[1],))


def back_dot(left, right):
    flat = left.reshape(-1, left.shape[-1])
    product = lax.dot_general(
        flat, right, (((1,), (1,)), ((), ())), preferred_element_type=jnp.float32
    )
    return product.reshape(left.shape[:-1] + (right.shape[0],))


def token_sum(left, right):
    left_rows = left.reshape(-1, left.shape[-1])
    right_rows = right.reshape(-1, right.shape[-1])
    return lax.dot_general(
        left_rows, right_rows, (((0,), (0,)), ((), ())), preferred_element_type=jnp.float32
    )


def split_join(joined):
    split_heads = joined.reshape(joined.shape[:-1] + (3, HEADS, HEAD_DIM))
    return (split_heads[..., 0, :, :], split_heads[..., 1, :, :], split_heads[..., 2, :, :])


def attend_core(normed, weight_in, token_form, key_form, score_form):
    joined = flat_dot(normed, weight_in).astype(jnp.bfloat16)
    queries, keyset, valueset = split_join(joined)
    factor = HEAD_DIM ** (-0.5)
    scores = (
        jnp.einsum(
            token_form + "hd," + key_form + "hd->" + score_form,
            queries,
            keyset,
            preferred_element_type=jnp.float32,
        )
        * factor
    )
    totals = jax.nn.logsumexp(scores, axis=-1, keepdims=True)
    weighting = jnp.exp(scores - totals).astype(jnp.bfloat16)
    context = jnp.einsum(
        score_form + "," + key_form + "hd->" + token_form + "hd",
        weighting,
        valueset,
        preferred_element_type=jnp.float32,
    )
    context = context.reshape(normed.shape[:-1] + (D,)).astype(jnp.bfloat16)
    return (joined, totals, context)


def attend_back(joined, totals, back_context, token_form, key_form, score_form):
    queries, keyset, valueset = split_join(joined)
    back_heads = back_context.reshape(back_context.shape[:-1] + (HEADS, HEAD_DIM))
    factor = HEAD_DIM ** (-0.5)
    scores = (
        jnp.einsum(
            token_form + "hd," + key_form + "hd->" + score_form,
            queries,
            keyset,
            preferred_element_type=jnp.float32,
        )
        * factor
    )
    weighting = jnp.exp(scores - totals)
    back_weight = jnp.einsum(
        token_form + "hd," + key_form + "hd->" + score_form,
        back_heads,
        valueset,
        preferred_element_type=jnp.float32,
    )
    back_weight = back_weight.astype(jnp.bfloat16).astype(jnp.float32)
    inner_sum = jnp.sum(weighting * back_weight, axis=-1, keepdims=True)
    back_scores = (weighting * (back_weight - inner_sum)).astype(jnp.bfloat16)
    back_query = (
        jnp.einsum(
            score_form + "," + key_form + "hd->" + token_form + "hd",
            back_scores,
            keyset,
            preferred_element_type=jnp.float32,
        )
        * factor
    )
    back_keys = (
        jnp.einsum(
            score_form + "," + token_form + "hd->" + key_form + "hd",
            back_scores,
            queries,
            preferred_element_type=jnp.float32,
        )
        * factor
    )
    back_values = jnp.einsum(
        score_form + "," + token_form + "hd->" + key_form + "hd",
        weighting.astype(jnp.bfloat16),
        back_heads,
        preferred_element_type=jnp.float32,
    )
    stacked = jnp.stack((back_query, back_keys, back_values), axis=-3)
    return stacked.reshape(back_context.shape[:-1] + (3 * D,)).astype(jnp.bfloat16)


def member_block(weights, gains, part, half):
    pieces = [lax.dynamic_slice_in_dim(w, part * half, half, axis=0) for w in weights[:5]]
    out_rows = lax.dynamic_slice_in_dim(weights[5], part * 4 * half, 4 * half, axis=0)
    pieces.append(jnp.concatenate([out_rows[q * half:(q + 1) * half] for q in range(4)], axis=1))
    gain_part = lax.dynamic_slice_in_dim(gains, part * half, half, axis=1).T
    pieces.append(jnp.pad(gain_part, ((0, 0), (0, GAIN_COLS - gain_part.shape[1]))))
    return jnp.concatenate(pieces, axis=1)


def unpack_rows(block, widths, half):
    members = block.shape[0] // half
    offsets = [0]
    for width in widths:
        offsets.append(offsets[-1] + width)
    outs = [block[:, offsets[i]:offsets[i + 1]] for i in range(5)]
    grouped = block[:, offsets[5]:offsets[6]].reshape(members, half, 4 * D)
    outs.append(
        jnp.concatenate([grouped[:, :, q * D:(q + 1) * D] for q in range(4)], axis=1).reshape(
            members * 4 * half, D
        )
    )
    outs.append(block[:, offsets[6]:offsets[6] + 3].T)
    return outs


def pack_grads(grads, gain_grads, members, half):
    pieces = [g.astype(jnp.bfloat16) for g in grads[:5]]
    grouped = grads[5].astype(jnp.bfloat16).reshape(members, 4 * half, D)
    pieces.append(
        jnp.concatenate([grouped[:, q * half:(q + 1) * half, :] for q in range(4)], axis=2).reshape(
            members * half, 4 * D
        )
    )
    gain_cols = gain_grads.T.astype(jnp.bfloat16)
    pieces.append(jnp.pad(gain_cols, ((0, 0), (0, GAIN_COLS - gain_cols.shape[1]))))
    return jnp.concatenate(pieces, axis=1)


def shards(
    inputs, space_in, space_out, time_in, time_out, hidden_in, hidden_out, norm_gains, cotangent
):
    weights = (space_in, space_out, time_in, time_out, hidden_in, hidden_out)
    widths = [w.shape[1] for w in weights[:5]] + [4 * D]
    fsdp_size = lax.axis_size("fsdp")
    core_size = lax.axis_size("core")
    members = fsdp_size * core_size
    half = space_in.shape[0] // core_size
    core = lax.axis_index("core")

    block = member_block(weights, norm_gains, core, half)
    gathered = lax.all_gather(block, MEMBERS, axis=0, tiled=True)
    s_in, s_out, t_in, t_out, h_in, h_out, gains = unpack_rows(gathered, widths, half)
    gain_rows = gains.astype(jnp.float32)

    micro, _, frames, places, _ = inputs.shape
    spatial = ("gl", "gm", "ghlm")
    temporal = ("blg", "bmg", "bghlm")

    frames_in = inputs[:, 0].astype(jnp.float32)
    normed_one = layer_norm(frames_in, gain_rows[0]).astype(jnp.bfloat16)
    join_space, total_space, context_space = attend_core(
        normed_one.reshape(micro * frames, places, D), s_in, *spatial
    )
    context_space = context_space.reshape(micro, frames, places, D)
    mixed_one = frames_in + flat_dot(context_space, s_out)
    normed_two = layer_norm(mixed_one, gain_rows[1]).astype(jnp.bfloat16)
    placed = lax.all_to_all(normed_two, "fsdp", split_axis=2, concat_axis=1, tiled=True)
    join_time, total_time, context_placed = attend_core(placed, t_in, *temporal)
    context_time = lax.all_to_all(context_placed, "fsdp", split_axis=1, concat_axis=2, tiled=True)
    mixed_two = mixed_one + flat_dot(context_time, t_out)
    normed_three = layer_norm(mixed_two, gain_rows[2]).astype(jnp.bfloat16)
    hidden = flat_dot(normed_three, h_in)
    activated = jax.nn.gelu(hidden, approximate=False).astype(jnp.bfloat16)
    result = mixed_two + flat_dot(activated, h_out)

    upstream = cotangent[:, 0].astype(jnp.float32)
    rounded = upstream.astype(jnp.bfloat16)
    grad_hidden_out = token_sum(activated, rounded)
    back_active = back_dot(rounded, h_out).astype(jnp.bfloat16)
    unused, gelu_pull = jax.vjp(partial(jax.nn.gelu, approximate=False), hidden)
    back_hidden = gelu_pull(back_active.astype(jnp.float32))[0].astype(jnp.bfloat16)
    grad_hidden_in = token_sum(normed_three, back_hidden)
    back_three = back_dot(back_hidden, h_in).astype(jnp.bfloat16)
    back_mixed, gain_grad_two = norm_back(mixed_two, gain_rows[2], back_three.astype(jnp.float32))
    upstream = upstream + back_mixed
    rounded = upstream.astype(jnp.bfloat16)
    grad_time_out = token_sum(context_time, rounded)
    back_context = back_dot(rounded, t_out).astype(jnp.bfloat16)
    back_placed = lax.all_to_all(back_context, "fsdp", split_axis=2, concat_axis=1, tiled=True)
    back_join = attend_back(join_time, total_time, back_placed, *temporal)
    grad_time_in = token_sum(placed, back_join)
    back_two_placed = back_dot(back_join, t_in).astype(jnp.bfloat16)
    back_two = lax.all_to_all(back_two_placed, "fsdp", split_axis=1, concat_axis=2, tiled=True)
    back_mixed, gain_grad_one = norm_back(mixed_one, gain_rows[1], back_two.astype(jnp.float32))
    upstream = upstream + back_mixed
    rounded = upstream.astype(jnp.bfloat16)
    grad_space_out = token_sum(context_space, rounded)
    back_context = back_dot(rounded, s_out).astype(jnp.bfloat16)
    back_join = attend_back(
        join_space, total_space, back_context.reshape(micro * frames, places, D), *spatial
    )
    grad_space_in = token_sum(normed_one, back_join)
    back_one = back_dot(back_join, s_in).astype(jnp.bfloat16).reshape(micro, frames, places, D)
    back_mixed, gain_grad_zero = norm_back(frames_in, gain_rows[0], back_one.astype(jnp.float32))
    input_grad = upstream + back_mixed

    grads = (grad_space_in, grad_space_out, grad_time_in, grad_time_out, grad_hidden_in, grad_hidden_out)
    gain_grads = jnp.stack((gain_grad_zero, gain_grad_one, gain_grad_two))
    packed = pack_grads(grads, gain_grads, members, half)
    owned = lax.psum_scatter(packed, MEMBERS, scatter_dimension=0, tiled=True)
    owned = lax.psum(owned, "dpo")
    owned = lax.all_gather(owned, "core", axis=0, tiled=True)
    outs = unpack_rows(owned, widths, half)
    outs = [part.astype(jnp.float32) for part in outs]
    return (result[:, None], input_grad[:, None], *outs)


def solution(mesh):
    dp_size, fsdp_size = mesh.devices.shape
    split = Mesh(mesh.devices.reshape(dp_size // 2, 2, fsdp_size), ("dpo", "core", "fsdp"))
    tokens = P(None, ("dpo", "core"), "fsdp", None, None)
    rows = P("fsdp", None)
    return jax.shard_map(
        shards,
        mesh=split,
        in_specs=(tokens, rows, rows, rows, rows, rows, rows, P(None, "fsdp"), tokens),
        out_specs=(tokens, tokens, rows, rows, rows, rows, rows, rows, P(None, "fsdp")),
        check_vma=False,
    )
```

time: 1210 us -> 829 us (0.69)
  waiting for transfers between devices: 771 us -> 375 us
  other arithmetic: 61.4 us -> 90.8 us
  starting transfers between devices: 39.2 us -> 13.3 us
  matrix products: 170 us -> 146 us
  local copies, waits for them, and re-layouts: 120 us -> 143 us
    reduce_scatter x6 -> x1, waiting for transfers between devices: 371 us -> 196 us  [shards(): owned = lax.psum_scatter(packed, MEMBERS, scatter_dimension=0, tiled=True)]
    all_gather x6 -> x2, waiting for transfers between devices: 213 us -> 99.8 us  [the longest x1 99.8 us: shards(): gathered = lax.all_gather(block, MEMBERS, axis=0, tiled=True)]
    unnamed x15 -> x4, waiting for transfers between devices: 63.4 us -> 0.07 us
    all_to_all x8 -> x3, waiting for transfers between devices: 73.7 us -> 34.1 us  [the longest x1 17.7 us: shards(): lax.all_to_all(back_context, 'fsdp', split_axis=2, concat_axis=1, tiled=T...]
    all_to_all x0 -> x1, blocking collectives: none -> 34 us  [shards(): lax.all_to_all(normed_two, 'fsdp', split_axis=2, concat_axis=1, tiled=True)]
    convert_element_type x13 -> x9, other arithmetic: 12 us -> 38.3 us  [the longest x1 26 us: shards(): gelu_pull(back_active.astype(jnp.float32))[0].astype(jnp.bfloat16)]
    convert_element_type x17 -> x15, local copies, waits for them, and re-layouts: 47.8 us -> 73 us  [the longest x6 49.5 us: attend_back(): stacked.reshape(back_context.shape[:-1] + (3 * D,)).astype(jnp.bfloat16)]
    all_to_all x8 -> x3, starting transfers between devices: 37.5 us -> 13.2 us  [the longest x1 4.46 us: shards(): lax.all_to_all(context_placed, 'fsdp', split_axis=1, concat_axis=2, tiled...]
  transfers between devices with their start and end apart: 22 -> 7, of which waited for: 17 -> 5; matrix products, arithmetic and copies ran while one was open for 22% -> 10% of each run, Pallas kernels for 0% -> 0%
where the time goes in v1:
time: 829 us; the launch traced here: 818 us
  waiting for transfers between devices  375 us (45%)
  matrix products  146 us (18%)
  local copies, waits for them, and re-layouts  143 us (17%)
  other arithmetic  90.8 us (11%)
  blocking collectives  34 us (4%)
  between operations  15.3 us (2%)
  starting transfers between devices  13.3 us (2%)
    reduce_scatter x1, waiting for transfers between devices, shards(): owned = lax.psum_scatter(packed, MEMBERS, scatter_dimension=0, tiled=True)  196 us
    all_gather x1, waiting for transfers between devices, shards(): gathered = lax.all_gather(block, MEMBERS, axis=0, tiled=True)  99.8 us
    convert_element_type x6, local copies, waits for them, and re-layouts, attend_back(): stacked.reshape(back_context.shape[:-1] + (3 * D,)).astype(jnp.bfloat16)  49.5 us
    psum x1, waiting for transfers between devices, shards(): owned = lax.psum(owned, 'dpo')  44.6 us
    dot_general x6, matrix products, flat_dot(): product = jnp.dot(flat, right, preferred_element_type=jnp.float32)  38.3 us
    all_to_all x1, blocking collectives, shards(): lax.all_to_all(normed_two, 'fsdp', split_axis=2, concat_axis=1, tiled=True)  34 us
    dot_general x6, matrix products, token_sum(): lax.dot_general(left_rows, right_rows, (((0,), (0,)), ((), ())), preferre...  32.3 us
    dot_general x6, matrix products, back_dot(): lax.dot_general(flat, right, (((1,), (1,)), ((), ())), preferred_element_...  30 us
  transfers between devices with their start and end apart: 7, of which 5 were waited for; matrix products, arithmetic and copies ran while one was open for 10% of the time, Pallas kernels for 0%

profile of v1, /device:TPU:0, one launch (start us, length us, event | category | flops | bytes accessed | tf_op | source)
XLA Modules:
  0.0 817.9 jit_solution(5993336394174902157)
XLA Ops:
  19.7 99.8 %all-gather.3.cloned.1.call-done = bf16[768,12416]{1,0:T(8,128)(2,1)} async-done(((bf16[48,12416]{1,0:T(8,128)(2,1)}), bf16[768,12416]{1,0:T(8,128)(2,1)}) %all-gather.3.cloned.1.call-update) | async-done | bytes 19070992 | tf_op jit(solution)/shard_map/all_gather | solution.py:184
  121.1 6.5 convolution_convert_fusion.3
  151.6 34.0 %all_to_all.54 = bf16[2,2,192,768]{3,1,0,2:T(2,128)(2,1)S(1)} all-to-all(bf16[2,2,192,768]{3,1,0,2:T(2,128)(2,1)S(1)} %copy.172), channel_id=1, replica_groups=mesh['dpo'=2,'core'=2,'fsdp'=8] {'fsdp'}, dimensions={2} | all-to-all | bytes 2359296 | tf_op jit(solution)/shard_map/all_to_all | solution.py:200
  191.4 11.6 %reshape.341 = bf16[2,16,24,3,12,64]{5,4,3,2,1,0:T(8,128)(2,1)} reshape(bf16[2,16,24,2304]{3,2,1,0:T(8,128)(2,1)} %convolution_convert_fusion.2) | data formatting | bytes 7077888 | tf_op jit(solution)/shard_map/reshape | solution.py:54
  238.8 16.4 %all-to-all-done.1 = bf16[2,16,24,768]{3,2,0,1:T(8,128)(2,1)} async-done(((bf16[2,16,24,768]{3,2,0,1:T(8,128)(2,1)}), bf16[2,16,24,768]{3,2,0,1:T(8,128)(2,1)}, u32[]{:S(2)}, u32[]{:S(2)}) %all-to-all-start.1) | async-done | bytes 1179680 | tf_op jit(solution)/shard_map/all_to_all | solution.py:202
  260.0 12.2 %fusion.43 = (u8[2,192,3072]{2,1,0:T(8,128)(4,1)S(1)}, u8[2,192,3072]{2,1,0:T(8,128)(4,1)S(1)}, f32[2,2,192,3072]{3,2,1,0:T(8,128)}) fusion(bf16[768,12416]{1,0:T(8,128)(2,1)} %all-gather.3.cloned.1.call-done, f32[2,2,192,768]{3,2,1,0:T(8,128)S(1)} %get-tuple-element.99, f32[768]{0:T(1024)S(1)} %get-tuple-element.62, f32[2,2,192]{2,1,0:T(2,128)S(1)} %fusion.61, ...), kind=kOutput, calls=%fused_computation.113 | convolution fusion | flops 3654549504 | bytes 18883584 | tf_op jit(solution)/shard_map/dot_general | solution.py:33
  272.2 26.0 %add_convert_fusion = (bf16[2,2,192,3072]{3,2,1,0:T(8,128)(2,1)S(1)}, f32[2,2,192,3072]{3,2,1,0:T(8,128)}) fusion(f32[2,2,192,3072]{3,2,1,0:T(8,128)} %bitcast.285, f32[2,2,192,3072]{3,2,1,0:T(8,128)} %get-tuple-element.100, u8[2,192,3072]{2,1,0:T(8,128)(4,1)S(1)} %get-tuple-element.55, u8[2,192,3072]{2,1,0:T(8,128)(4,1)S(1)} %get-tuple-element.54), kind=kLoop, calls=%fused_computation.15 | loop fusion | flops 181665792 | bytes 35389440 | tf_op jit(solution)/shard_map/convert_element_type | solution.py:214
  298.3 8.1 fusion.24
  327.8 17.7 %all-to-all-done.2 = bf16[2,2,192,768]{3,1,0,2:T(2,128)(2,1)} async-done(((bf16[2,2,192,768]{3,1,0,2:T(2,128)(2,1)}), bf16[2,2,192,768]{3,1,0,2:T(2,128)(2,1)}, u32[]{:S(2)}, u32[]{:S(2)}) %all-to-all-start.2) | async-done | bytes 1179680 | tf_op jit(solution)/shard_map/all_to_all | solution.py:222
  352.6 8.3 %fusion.14 = (f32[2,24,12,16]{3,2,1,0:T(8,128)S(1)}, bf16[2,24,12,16,16]{3,4,2,1,0:T(8,128)(2,1)S(1)}) fusion(f32[2,24,12,16,16]{3,4,2,1,0:T(8,128)} %copy-done.3, f32[2,24,12,16]{3,2,1,0:T(8,128)S(1)} %log_add_fusion, bf16[2,16,24,1,12,64]{5,4,3,2,1,0:T(8,128)(2,1)} %copy-done.16, bf16[2,16,24,12,64]{4,3,2,1,0:T(8,128)(2,1)} %reshape.345), kind=kOutput, calls=%fused_computation.45 | convolution fusion | flops 19749888 | bytes 3317760 | tf_op jit(solution)/shard_map/blghd,bmghd->bghlm/dot_general | solution.py:97
  372.9 9.2 %copy.189 = bf16[2,16,24,3,12,64]{5,4,3,2,1,0:T(8,128)(2,1)} copy(bf16[2,16,24,3,12,64]{5,1,4,2,0,3:T(8,128)(2,1)} %maximum_convert_fusion) | data formatting | bytes 7077888 | tf_op jit(solution)/shard_map/convert_element_type | solution.py:131
  382.2 12.0 %convert_element_type.287 = bf16[2,16,24,2304]{3,2,1,0:T(8,128)(2,1)} reshape(bf16[2,16,24,3,12,64]{5,4,3,2,1,0:T(8,128)(2,1)} %copy.189) | data formatting | bytes 7077888 | tf_op jit(solution)/shard_map/convert_element_type | solution.py:131
  405.6 10.9 %multiply_convert_fusion = bf16[2,2,192,3072]{3,2,1,0:T(8,128)(2,1)} fusion(f32[2,2,192,3072]{3,2,1,0:T(8,128)} %get-tuple-element.68, f32[2,2,192,3072]{3,2,1,0:T(8,128)} %get-tuple-element.100), kind=kLoop, calls=%fused_computation.16 | loop fusion | flops 7077888 | bytes 23592960 | tf_op jit(solution)/shard_map/convert_element_type | solution.py:206
  423.6 6.6 convolution_convert_fusion.4
  433.1 12.0 %convert_element_type.310 = bf16[768,2304]{1,0:T(8,128)(2,1)} reshape(bf16[2,16,24,3,12,64]{5,4,3,2,1,0:T(8,128)(2,1)} %copy.189) | data formatting | bytes 7077888 | tf_op jit(solution)/shard_map/convert_element_type | solution.py:131
  456.9 8.0 fusion
  465.0 10.4 %fusion.2 = bf16[4,12,192,192]{2,3,1,0:T(8,128)(2,1)} fusion(bf16[4,12,192,192]{2,3,1,0:T(8,128)(2,1)} %get-tuple-element.106, f32[4,12,192,192]{2,3,1,0:T(8,128)} %copy-done.2, f32[4,12,192]{2,1,0:T(8,128)S(1)} %get-tuple-element.105, f32[4,12,192]{2,1,0:T(8,128)S(1)} %copy-done.33), kind=kLoop, calls=%fused_computation.6 | loop fusion | flops 10616832 | bytes 14229504 | tf_op jit(solution)/shard_map/convert_element_type | solution.py:105
  487.8 6.6 copy.198
  504.5 9.1 %convert_element_type.306 = bf16[768,2304]{0,1:T(8,128)(2,1)} reshape(bf16[4,192,3,12,64]{1,0,4,3,2:T(4,128)(2,1)} %copy.198) | data formatting | bytes 7077888 | tf_op jit(solution)/shard_map/convert_element_type | solution.py:131
  517.4 7.0 fusion.11
  531.8 8.3 %fusion.12 = bf16[768,12416]{1,0:T(8,128)(2,1)} fusion(bf16[768,12416]{1,0:T(8,128)(2,1)} %constant_dynamic-update-slice_fusion.2, bf16[2,2,192,3072]{3,2,1,0:T(8,128)(2,1)} %copy-done.22, f32[2,2,192,768]{3,2,1,0:T(8,128)S(1)} %copy-done.6, f32[768]{0:T(1024)S(1)} %copy-done.44, f32[2,2,192]{2,1,0:T(2,128)S(1)} %copy-done.46, ...), kind=kOutput, calls=%fused_computation.41 | convolution fusion | flops 3628597248 | bytes 11805696 | tf_op jit(solution)/shard_map/dot_general | solution.py:48
  543.4 196.3 %reduce-scatter.2.cloned.1.call-done = bf16[48,12416]{1,0:T(8,128)(2,1)} async-done(((bf16[768,12416]{1,0:T(8,128)(2,1)}), bf16[48,12416]{1,0:T(8,128)(2,1)}) %reduce-scatter.2.cloned.1.call-update) | async-done | bytes 1191952 | tf_op jit(solution)/shard_map/reduce_scatter | solution.py:243
  739.8 44.6 %all-reduce.4.cloned.1.call-done = bf16[48,12416]{1,0:T(8,128)(2,1)} async-done(((bf16[48,12416]{1,0:T(8,128)(2,1)}), bf16[48,12416]{1,0:T(8,128)(2,1)}) %all-reduce.4.cloned.1.call-update) | async-done | bytes 1191952 | tf_op jit(solution)/shard_map/psum | solution.py:244
  784.5 9.0 %add_bitcast_fusion = f32[2,1,2,192,768]{4,3,2,1,0:T(8,128)} fusion(f32[2,2,192,768]{3,2,1,0:T(8,128)S(1)} %copy-done.6, bf16[2,2,192,3072]{3,2,1,0:T(8,128)(2,1)} %multiply_convert_fusion, bf16[3072,768,1,1]{1,0,3,2:T(8,128)(2,1)} %bitcast.289), kind=kOutput, calls=%fused_computation.105 | convolution fusion | flops 3624468480 | bytes 14155776 | tf_op jit(solution)/shard_map/dot_general | solution.py:33
  (282 shorter events, 211.9 us)
Async XLA Ops:
  7.2 112.3 %all-gather.3.cloned.1.call-start = ((), (), s32[]{:S(2)}) async-start(), calls=%async_computation.5 | async-start | bytes 20262912 | tf_op jit(solution)/shard_map/all_gather | solution.py:184
  19.7 107.9 %copy-start.20 = (f32[4,192,768]{2,1,0:T(8,128)}, f32[4,192,768]{2,1,0:T(8,128)S(1)}, u32[]{:S(2)}) copy-start(f32[4,192,768]{2,1,0:T(8,128)S(1)} %bitcast_subtract_fusion) | copy-start | bytes 7077892
  121.1 28.9 %copy-start.47 = (f32[768]{0:T(1024)}, f32[768]{0:T(1024)S(1)}, u32[]{:S(2)}) copy-start(f32[768]{0:T(1024)S(1)} %get-tuple-element.63) | copy-start | bytes 9220
  121.1 186.7 %copy-start.42 = (f32[768]{0:T(1024)}, f32[768]{0:T(1024)S(1)}, u32[]{:S(2)}) copy-start(f32[768]{0:T(1024)S(1)} %get-tuple-element.62) | copy-start | bytes 9220
  137.3 49.6 %slice-start.7 = ((s8[19070976]{0:T(1024)(128)(4,1)}), s8[2293760]{0:T(1024)(128)(4,1)S(1)}, s32[]{:S(2)}) async-start(s8[19070976]{0:T(1024)(128)(4,1)} %bitcast.278), calls=%async_computation.16 | async-start | bytes 4587520
  137.3 49.6 %slice-start.8 = ((s8[19070976]{0:T(1024)(128)(4,1)}), s8[4194304]{0:T(1024)(128)(4,1)S(1)}, s32[]{:S(2)}) async-start(s8[19070976]{0:T(1024)(128)(4,1)} %bitcast.278), calls=%async_computation.17 | async-start | bytes 8388608
  142.1 44.9 %slice-start.9 = ((s8[19070976]{0:T(1024)(128)(4,1)}), s8[4194304]{0:T(1024)(128)(4,1)S(1)}, s32[]{:S(2)}) async-start(s8[19070976]{0:T(1024)(128)(4,1)} %bitcast.278), calls=%async_computation.18 | async-start | bytes 8388608
  146.3 40.6 %slice-start.10 = ((s8[19070976]{0:T(1024)(128)(4,1)}), s8[4194304]{0:T(1024)(128)(4,1)S(1)}, s32[]{:S(2)}) async-start(s8[19070976]{0:T(1024)(128)(4,1)} %bitcast.278), calls=%async_computation.19 | async-start | bytes 8388608
  150.3 36.6 %slice-start.11 = ((s8[19070976]{0:T(1024)(128)(4,1)}), s8[4194304]{0:T(1024)(128)(4,1)S(1)}, s32[]{:S(2)}) async-start(s8[19070976]{0:T(1024)(128)(4,1)} %bitcast.278), calls=%async_computation.20 | async-start | bytes 8388608
  222.9 32.4 %all-to-all-start.1 = ((bf16[2,16,24,768]{3,2,0,1:T(8,128)(2,1)}), bf16[2,16,24,768]{3,2,0,1:T(8,128)(2,1)}, u32[]{:S(2)}, u32[]{:S(2)}) async-start(bf16[2,16,24,768]{3,2,0,1:T(8,128)(2,1)} %reshape.368), calls=%async_computation.1 | async-start | bytes 2359296 | tf_op jit(solution)/shard_map/all_to_all | solution.py:202
  259.5 48.3 %copy-start.4 = (f32[2,2,192,768]{3,2,1,0:T(8,128)}, f32[2,2,192,768]{3,2,1,0:T(8,128)S(1)}, u32[]{:S(2)}) copy-start(f32[2,2,192,768]{3,2,1,0:T(8,128)S(1)} %get-tuple-element.99) | copy-start | bytes 7077892
  260.0 188.9 %copy-start.45 = (f32[2,2,192]{2,1,0:T(2,128)}, f32[2,2,192]{2,1,0:T(2,128)S(1)}, u32[]{:S(2)}) copy-start(f32[2,2,192]{2,1,0:T(2,128)S(1)} %fusion.61) | copy-start | bytes 9220
  298.2 10.9 %slice-start.12 = ((s8[19070976]{0:T(1024)(128)(4,1)}), s8[2293760]{0:T(1024)(128)(4,1)S(1)}, s32[]{:S(2)}) async-start(s8[19070976]{0:T(1024)(128)(4,1)} %bitcast.280), calls=%async_computation.21 | async-start | bytes 4587520
  298.3 10.9 %slice-start.13 = ((s8[19070976]{0:T(1024)(128)(4,1)}), s8[4194304]{0:T(1024)(128)(4,1)S(1)}, s32[]{:S(2)}) async-start(s8[19070976]{0:T(1024)(128)(4,1)} %bitcast.280), calls=%async_computation.22 | async-start | bytes 8388608
  298.3 10.9 %slice-start.14 = ((s8[19070976]{0:T(1024)(128)(4,1)}), s8[4194304]{0:T(1024)(128)(4,1)S(1)}, s32[]{:S(2)}) async-start(s8[19070976]{0:T(1024)(128)(4,1)} %bitcast.280), calls=%async_computation.23 | async-start | bytes 8388608
  312.8 32.6 %all-to-all-start.2 = ((bf16[2,2,192,768]{3,1,0,2:T(2,128)(2,1)}), bf16[2,2,192,768]{3,1,0,2:T(2,128)(2,1)}, u32[]{:S(2)}, u32[]{:S(2)}) async-start(bf16[2,2,192,768]{3,1,0,2:T(2,128)(2,1)} %copy.184), calls=%async_computation.2 | async-start | bytes 2359296 | tf_op jit(solution)/shard_map/all_to_all | solution.py:222
  347.9 13.1 %slice-start.3 = ((s8[4718592]{0:T(1024)(128)(4,1)}), s8[524288]{0:T(1024)(128)(4,1)S(1)}, s32[]{:S(2)}) async-start(s8[4718592]{0:T(1024)(128)(4,1)} %bitcast.267), calls=%async_computation.12 | async-start | bytes 1048576
  401.3 43.8 %all-to-all-start.3 = ((bf16[2,16,24,768]{3,2,0,1:T(8,128)(2,1)}), bf16[2,16,24,768]{3,2,0,1:T(8,128)(2,1)}, u32[]{:S(2)}, u32[]{:S(2)}) async-start(bf16[2,16,24,768]{3,2,0,1:T(8,128)(2,1)} %copy.190), calls=%async_computation.3 | async-start | bytes 2359296 | tf_op jit(solution)/shard_map/all_to_all | solution.py:226
  405.5 334.3 %reduce-scatter.2.cloned.1.call-start = ((), (), s32[]{:S(2)}) async-start(), calls=%async_computation.6 | async-start | bytes 20262912 | tf_op jit(solution)/shard_map/reduce_scatter | solution.py:243
  465.0 18.8 %slice-start = ((s8[9437184]{0:T(1024)(128)(4,1)}), s8[4194304]{0:T(1024)(128)(4,1)S(1)}, s32[]{:S(2)}) async-start(s8[9437184]{0:T(1024)(128)(4,1)} %bitcast.265), calls=%async_computation.9 | async-start | bytes 8388608
  465.0 18.8 %slice-start.1 = ((s8[9437184]{0:T(1024)(128)(4,1)}), s8[1048576]{0:T(1024)(128)(4,1)S(1)}, s32[]{:S(2)}) async-start(s8[9437184]{0:T(1024)(128)(4,1)} %bitcast.265), calls=%async_computation.10 | async-start | bytes 2097152
  526.1 14.0 %slice-start.5 = ((s8[4718592]{0:T(1024)(128)(4,1)}), s8[4194304]{0:T(1024)(128)(4,1)S(1)}, s32[]{:S(2)}) async-start(s8[4718592]{0:T(1024)(128)(4,1)} %bitcast.275), calls=%async_computation.14 | async-start | bytes 8388608
  543.4 241.0 %all-reduce.4.cloned.1.call-start = ((), (), s32[]{:S(2)}) async-start(), calls=%async_computation.7 | async-start | bytes 2383872 | tf_op jit(solution)/shard_map/psum | solution.py:244
  739.8 63.8 %all-gather.5.cloned.1.call-start = ((), (), s32[]{:S(2)}) async-start(), calls=%async_computation.8 | async-start | bytes 3575808 | tf_op jit(solution)/shard_map/all_gather | solution.py:245
  (56 other events, 222.0 us)
Sparse Core Ops, SparseCore 0:
  17.0 102.5 all-gather.2
  543.5 196.2 reduce-scatter.1
  742.1 42.3 all-reduce.3
  785.8 11.0 all-gather.4

commit v2 on v1

--- a/solution.py
+++ b/solution.py
@@ -6,6 +6,7 @@
 from jax.sharding import Mesh
 from jax.sharding import PartitionSpec as P
 
+
 D = 768
 HEADS = 12
 HEAD_DIM = 64
@@ -24,7 +25,7 @@
 
 
 def norm_back(values, scales, incoming):
-    unused, pullback = jax.vjp(layer_norm, values, scales)
+    _, pullback = jax.vjp(layer_norm, values, scales)
     return pullback(incoming)
 
 
@@ -131,58 +132,108 @@
     return stacked.reshape(back_context.shape[:-1] + (3 * D,)).astype(jnp.bfloat16)
 
 
-def member_block(weights, gains, part, half):
-    pieces = [lax.dynamic_slice_in_dim(w, part * half, half, axis=0) for w in weights[:5]]
-    out_rows = lax.dynamic_slice_in_dim(weights[5], part * 4 * half, 4 * half, axis=0)
-    pieces.append(jnp.concatenate([out_rows[q * half:(q + 1) * half] for q in range(4)], axis=1))
-    gain_part = lax.dynamic_slice_in_dim(gains, part * half, half, axis=1).T
-    pieces.append(jnp.pad(gain_part, ((0, 0), (0, GAIN_COLS - gain_part.shape[1]))))
-    return jnp.concatenate(pieces, axis=1)
-
-
-def unpack_rows(block, widths, half):
+def to_member(array, kind, part, half):
+    if kind == "gains":
+        gain_part = lax.dynamic_slice_in_dim(array, part * half, half, axis=1).T
+        return jnp.pad(gain_part, ((0, 0), (0, GAIN_COLS - gain_part.shape[1])))
+    if kind == "grouped":
+        rows = lax.dynamic_slice_in_dim(array, part * 4 * half, 4 * half, axis=0)
+        return jnp.concatenate([rows[q * half:(q + 1) * half] for q in range(4)], axis=1)
+    return lax.dynamic_slice_in_dim(array, part * half, half, axis=0)
+
+
+def width_of(array, kind):
+    return {"gains": GAIN_COLS, "grouped": 4 * D}.get(kind, array.shape[-1])
+
+
+def from_members(block, kinds, widths, half):
     members = block.shape[0] // half
-    offsets = [0]
-    for width in widths:
-        offsets.append(offsets[-1] + width)
-    outs = [block[:, offsets[i]:offsets[i + 1]] for i in range(5)]
-    grouped = block[:, offsets[5]:offsets[6]].reshape(members, half, 4 * D)
-    outs.append(
-        jnp.concatenate([grouped[:, :, q * D:(q + 1) * D] for q in range(4)], axis=1).reshape(
-            members * 4 * half, D
-        )
-    )
-    outs.append(block[:, offsets[6]:offsets[6] + 3].T)
+    outs = []
+    offset = 0
+    for kind, width in zip(kinds, widths):
+        part = block[:, offset:offset + width]
+        offset += width
+        if kind == "gains":
+            outs.append(part[:, :3].T)
+        elif kind == "grouped":
+            grouped = part.reshape(members, half, 4 * D)
+            outs.append(
+                jnp.concatenate([grouped[:, :, q * D:(q + 1) * D] for q in range(4)], axis=1).reshape(
+                    members * 4 * half, D
+                )
+            )
+        else:
+            outs.append(part)
     return outs
 
 
-def pack_grads(grads, gain_grads, members, half):
-    pieces = [g.astype(jnp.bfloat16) for g in grads[:5]]
-    grouped = grads[5].astype(jnp.bfloat16).reshape(members, 4 * half, D)
-    pieces.append(
-        jnp.concatenate([grouped[:, q * half:(q + 1) * half, :] for q in range(4)], axis=2).reshape(
-            members * half, 4 * D
-        )
-    )
-    gain_cols = gain_grads.T.astype(jnp.bfloat16)
-    pieces.append(jnp.pad(gain_cols, ((0, 0), (0, GAIN_COLS - gain_cols.shape[1]))))
-    return jnp.concatenate(pieces, axis=1)
-
-
-def shards(
+def to_members_full(array, kind, members, half):
+    array = array.astype(jnp.bfloat16)
+    if kind == "gains":
+        cols = array.T
+        return jnp.pad(cols, ((0, 0), (0, GAIN_COLS - cols.shape[1])))
+    if kind == "grouped":
+        grouped = array.reshape(members, 4 * half, D)
+        return jnp.concatenate(
+            [grouped[:, q * half:(q + 1) * half, :] for q in range(4)], axis=2
+        ).reshape(members * half, 4 * D)
+    return array
+
+
+def gather_group(arrays, kinds, part, half):
+    block = jnp.concatenate([to_member(a, k, part, half) for a, k in zip(arrays, kinds)], axis=1)
+    widths = [width_of(a, k) for a, k in zip(arrays, kinds)]
+    gathered = lax.all_gather(block, MEMBERS, axis=0, tiled=True)
+    return from_members(gathered, kinds, widths, half)
+
+
+def pair_sum(values, axis):
+    if lax.axis_size(axis) == 2:
+        return values + lax.ppermute(values, axis, [(0, 1), (1, 0)])
+    return lax.psum(values, axis)
+
+
+def core_gather(values):
+    if lax.axis_size("core") == 2:
+        other = lax.ppermute(values, "core", [(0, 1), (1, 0)])
+        first = lax.axis_index("core") == 0
+        return jnp.concatenate(
+            [jnp.where(first, values, other), jnp.where(first, other, values)], axis=0
+        )
+    return lax.all_gather(values, "core", axis=0, tiled=True)
+
+
+def pack_group(grads, kinds, members, half):
+    return jnp.concatenate(
+        [to_members_full(g, k, members, half) for g, k in zip(grads, kinds)], axis=1
+    )
+
+
+def reduce_group(packed, grads, kinds, half):
+    widths = [width_of(g, k) for g, k in zip(grads, kinds)]
+    owned = lax.psum_scatter(packed, MEMBERS, scatter_dimension=0, tiled=True)
+    owned = core_gather(pair_sum(owned, "dpo"))
+    return [part.astype(jnp.float32) for part in from_members(owned, kinds, widths, half)]
+
+
+def layer(
     inputs, space_in, space_out, time_in, time_out, hidden_in, hidden_out, norm_gains, cotangent
 ):
-    weights = (space_in, space_out, time_in, time_out, hidden_in, hidden_out)
-    widths = [w.shape[1] for w in weights[:5]] + [4 * D]
     fsdp_size = lax.axis_size("fsdp")
     core_size = lax.axis_size("core")
     members = fsdp_size * core_size
     half = space_in.shape[0] // core_size
     core = lax.axis_index("core")
 
-    block = member_block(weights, norm_gains, core, half)
-    gathered = lax.all_gather(block, MEMBERS, axis=0, tiled=True)
-    s_in, s_out, t_in, t_out, h_in, h_out, gains = unpack_rows(gathered, widths, half)
+    s_in, s_out, gains = gather_group(
+        (space_in, space_out, norm_gains), ("plain", "plain", "gains"), core, half
+    )
+    t_in, t_out, h_in, h_out = gather_group(
+        (time_in, time_out, hidden_in, hidden_out),
+        ("plain", "plain", "plain", "grouped"),
+        core,
+        half,
+    )
     gain_rows = gains.astype(jnp.float32)
 
     micro, _, frames, places, _ = inputs.shape
@@ -210,10 +261,16 @@
     rounded = upstream.astype(jnp.bfloat16)
     grad_hidden_out = token_sum(activated, rounded)
     back_active = back_dot(rounded, h_out).astype(jnp.bfloat16)
-    unused, gelu_pull = jax.vjp(partial(jax.nn.gelu, approximate=False), hidden)
+    _, gelu_pull = jax.vjp(partial(jax.nn.gelu, approximate=False), hidden)
     back_hidden = gelu_pull(back_active.astype(jnp.float32))[0].astype(jnp.bfloat16)
     grad_hidden_in = token_sum(normed_three, back_hidden)
     back_three = back_dot(back_hidden, h_in).astype(jnp.bfloat16)
+    ffn_grads = (grad_hidden_in, grad_hidden_out)
+    ffn_kinds = ("plain", "grouped")
+    packed_ffn, back_three = lax.optimization_barrier(
+        (pack_group(ffn_grads, ffn_kinds, members, half), back_three)
+    )
+    grad_ffn = reduce_group(packed_ffn, ffn_grads, ffn_kinds, half)
     back_mixed, gain_grad_two = norm_back(mixed_two, gain_rows[2], back_three.astype(jnp.float32))
     upstream = upstream + back_mixed
     rounded = upstream.astype(jnp.bfloat16)
@@ -223,6 +280,12 @@
     back_join = attend_back(join_time, total_time, back_placed, *temporal)
     grad_time_in = token_sum(placed, back_join)
     back_two_placed = back_dot(back_join, t_in).astype(jnp.bfloat16)
+    time_grads = (grad_time_in, grad_time_out)
+    time_kinds = ("plain", "plain")
+    packed_time, back_two_placed = lax.optimization_barrier(
+        (pack_group(time_grads, time_kinds, members, half), back_two_placed)
+    )
+    grad_time = reduce_group(packed_time, time_grads, time_kinds, half)
     back_two = lax.all_to_all(back_two_placed, "fsdp", split_axis=1, concat_axis=2, tiled=True)
     back_mixed, gain_grad_one = norm_back(mixed_one, gain_rows[1], back_two.astype(jnp.float32))
     upstream = upstream + back_mixed
@@ -237,15 +300,23 @@
     back_mixed, gain_grad_zero = norm_back(frames_in, gain_rows[0], back_one.astype(jnp.float32))
     input_grad = upstream + back_mixed
 
-    grads = (grad_space_in, grad_space_out, grad_time_in, grad_time_out, grad_hidden_in, grad_hidden_out)
     gain_grads = jnp.stack((gain_grad_zero, gain_grad_one, gain_grad_two))
-    packed = pack_grads(grads, gain_grads, members, half)
-    owned = lax.psum_scatter(packed, MEMBERS, scatter_dimension=0, tiled=True)
-    owned = lax.psum(owned, "dpo")
-    owned = lax.all_gather(owned, "core", axis=0, tiled=True)
-    outs = unpack_rows(owned, widths, half)
-    outs = [part.astype(jnp.float32) for part in outs]
-    return (result[:, None], input_grad[:, None], *outs)
+    space_grads = (grad_space_in, grad_space_out, gain_grads)
+    space_kinds = ("plain", "plain", "gains")
+    grad_space = reduce_group(
+        pack_group(space_grads, space_kinds, members, half), space_grads, space_kinds, half
+    )
+    return (
+        result[:, None],
+        input_grad[:, None],
+        grad_space[0],
+        grad_space[1],
+        grad_time[0],
+        grad_time[1],
+        grad_ffn[0],
+        grad_ffn[1],
+        grad_space[2],
+    )
 
 
 def solution(mesh):
@@ -254,7 +325,7 @@
     tokens = P(None, ("dpo", "core"), "fsdp", None, None)
     rows = P("fsdp", None)
     return jax.shard_map(
-        shards,
+        layer,
         mesh=split,
         in_specs=(tokens, rows, rows, rows, rows, rows, rows, P(None, "fsdp"), tokens),
         out_specs=(tokens, tokens, rows, rows, rows, rows, rows, rows, P(None, "fsdp")),

time: 829 us -> 800 us (0.965)
  waiting for transfers between devices: 375 us -> 322 us
  blocking collectives: 34 us -> 57.9 us
  other arithmetic: 90.8 us -> 103 us
  local copies, waits for them, and re-layouts: 143 us -> 132 us
    psum x1 -> x0, waiting for transfers between devices: 44.6 us -> none  [shards(): owned = lax.psum(owned, 'dpo')]
    reduce_scatter x1 -> x3, waiting for transfers between devices: 196 us -> 154 us  [reduce_group(): owned = lax.psum_scatter(packed, MEMBERS, scatter_dimension=0, tiled=True)]
    all_to_all x3, waiting for transfers between devices: 34.1 us -> 59.9 us  [the longest x1 24.6 us: layer(): lax.all_to_all(back_context, 'fsdp', split_axis=2, concat_axis=1, tiled=T...]
    ppermute x0 -> x6, waiting for transfers between devices: none -> 24.3 us  [the longest x3 24.3 us: pair_sum(): return values + lax.ppermute(values, axis, [(0, 1), (1, 0)])]
    all_to_all x1, blocking collectives: 34 us -> 57.9 us  [layer(): lax.all_to_all(normed_two, 'fsdp', split_axis=2, concat_axis=1, tiled=True)]
    all_gather x2, waiting for transfers between devices: 99.8 us -> 83.2 us  [gather_group(): gathered = lax.all_gather(block, MEMBERS, axis=0, tiled=True)]
    concatenate x3 -> x8, other arithmetic: 2.89 us -> 12.6 us  [the longest x3 9.68 us: pack_group(): jnp.concatenate([to_members_full(g, k, members, half) for g, k in zip(gra...]
    unnamed x158 -> x140, local copies, waits for them, and re-layouts: 28.2 us -> 20.3 us
  transfers between devices with their start and end apart: 7 -> 14, of which waited for: 5 -> 10; matrix products, arithmetic and copies ran while one was open for 10% -> 20% of each run, Pallas kernels for 0% -> 0%
where the time goes in v2:
time: 800 us; the launch traced here: 794 us
  waiting for transfers between devices  322 us (40%)
  matrix products  146 us (18%)
  local copies, waits for them, and re-layouts  132 us (16%)
  other arithmetic  103 us (13%)
  blocking collectives  57.9 us (7%)
  starting transfers between devices  17.9 us (2%)
  between operations  15.2 us (2%)
    reduce_scatter x3, waiting for transfers between devices, reduce_group(): owned = lax.psum_scatter(packed, MEMBERS, scatter_dimension=0, tiled=True)  154 us
    all_gather x2, waiting for transfers between devices, gather_group(): gathered = lax.all_gather(block, MEMBERS, axis=0, tiled=True)  83.2 us
    all_to_all x1, blocking collectives, layer(): lax.all_to_all(normed_two, 'fsdp', split_axis=2, concat_axis=1, tiled=True)  57.9 us
    convert_element_type x6, local copies, waits for them, and re-layouts, attend_back(): stacked.reshape(back_context.shape[:-1] + (3 * D,)).astype(jnp.bfloat16)  51.2 us
    dot_general x6, matrix products, flat_dot(): product = jnp.dot(flat, right, preferred_element_type=jnp.float32)  39.6 us
    dot_general x6, matrix products, back_dot(): lax.dot_general(flat, right, (((1,), (1,)), ((), ())), preferred_element_...  31.6 us
    dot_general x6, matrix products, token_sum(): lax.dot_general(left_rows, right_rows, (((0,), (0,)), ((), ())), preferre...  28.4 us
    convert_element_type x1, other arithmetic, layer(): gelu_pull(back_active.astype(jnp.float32))[0].astype(jnp.bfloat16)  26.4 us
  transfers between devices with their start and end apart: 14, of which 10 were waited for; matrix products, arithmetic and copies ran while one was open for 20% of the time, Pallas kernels for 0%

profile of v2, /device:TPU:0, one launch (start us, length us, event | category | flops | bytes accessed | tf_op | source)
XLA Modules:
  0.0 793.5 jit_solution(17390704894462322932)
XLA Ops:
  21.3 46.4 %all-gather.3.cloned.1.call-done = bf16[768,3200]{1,0:T(8,128)(2,1)} async-done(((bf16[48,3200]{1,0:T(8,128)(2,1)}), bf16[768,3200]{1,0:T(8,128)(2,1)}) %all-gather.3.cloned.1.call-update) | async-done | bytes 4915216 | tf_op jit(solution)/shard_map/all_gather | solution.py:186
  69.3 7.5 convolution_convert_fusion.3
  99.8 57.9 %all_to_all.54 = bf16[2,2,192,768]{3,1,0,2:T(2,128)(2,1)S(1)} all-to-all(bf16[2,2,192,768]{3,1,0,2:T(2,128)(2,1)S(1)} %copy.172), channel_id=1, replica_groups=mesh['dpo'=2,'core'=2,'fsdp'=8] {'fsdp'}, dimensions={2} | all-to-all | bytes 2359296 | tf_op jit(solution)/shard_map/all_to_all | solution.py:251
  158.0 36.8 %all-gather.5.cloned.1.call-done = bf16[768,9216]{1,0:T(8,128)(2,1)} async-done(((bf16[48,9216]{1,0:T(8,128)(2,1)}), bf16[768,9216]{1,0:T(8,128)(2,1)}) %all-gather.5.cloned.1.call-update) | async-done | bytes 14155792 | tf_op jit(solution)/shard_map/all_gather | solution.py:186
  201.1 11.5 %reshape.341 = bf16[2,16,24,3,12,64]{5,4,3,2,1,0:T(8,128)(2,1)} reshape(bf16[2,16,24,2304]{3,2,1,0:T(8,128)(2,1)} %convolution_convert_fusion.2) | data formatting | bytes 7077888 | tf_op jit(solution)/shard_map/reshape | solution.py:55
  247.6 17.7 %all-to-all-done.1 = bf16[2,16,24,768]{3,2,0,1:T(8,128)(2,1)S(1)} async-done(((bf16[2,16,24,768]{3,2,0,1:T(8,128)(2,1)}), bf16[2,16,24,768]{3,2,0,1:T(8,128)(2,1)S(1)}, u32[]{:S(2)}, u32[]{:S(2)}) %all-to-all-start.1) | async-done | bytes 1179680 | tf_op jit(solution)/shard_map/all_to_all | solution.py:253
  269.5 10.0 %fusion.42 = (u8[2,192,3072]{2,1,0:T(8,128)(4,1)S(1)}, u8[2,192,3072]{2,1,0:T(8,128)(4,1)}, f32[2,2,192,3072]{3,2,1,0:T(8,128)S(1)}) fusion(bf16[768,9216]{1,0:T(8,128)(2,1)} %all-gather.5.cloned.1.call-done, f32[2,2,192,768]{3,2,1,0:T(8,128)S(1)} %get-tuple-element.109, f32[768]{0:T(1024)S(1)} %get-tuple-element.70, f32[2,2,192]{2,1,0:T(2,128)S(1)} %fusion.71, ...), kind=kOutput, calls=%fused_computation.115 | convolution fusion | flops 3654549504 | bytes 18883584 | tf_op jit(solution)/shard_map/dot_general | solution.py:34
  279.6 26.4 %add_convert_fusion = (bf16[2,2,192,3072]{3,2,1,0:T(8,128)(2,1)S(1)}, f32[2,2,192,3072]{3,2,1,0:T(8,128)}) fusion(f32[2,2,192,3072]{3,2,1,0:T(8,128)} %bitcast.277, f32[2,2,192,3072]{3,2,1,0:T(8,128)S(1)} %get-tuple-element.110, u8[2,192,3072]{2,1,0:T(8,128)(4,1)} %get-tuple-element.63, u8[2,192,3072]{2,1,0:T(8,128)(4,1)S(1)} %get-tuple-element.62), kind=kLoop, calls=%fused_computation.18 | loop fusion | flops 181665792 | bytes 35389440 | tf_op jit(solution)/shard_map/convert_element_type | solution.py:265
  312.4 10.9 %multiply_convert_fusion = bf16[2,2,192,3072]{3,2,1,0:T(8,128)(2,1)} fusion(f32[2,2,192,3072]{3,2,1,0:T(8,128)} %get-tuple-element.76, f32[2,2,192,3072]{3,2,1,0:T(8,128)} %copy-done.9), kind=kLoop, calls=%fused_computation.19 | loop fusion | flops 7077888 | bytes 23592960 | tf_op jit(solution)/shard_map/convert_element_type | solution.py:257
  336.8 7.8 fusion.49
  360.5 24.6 %all-to-all-done.2 = bf16[2,2,192,768]{3,1,0,2:T(2,128)(2,1)} async-done(((bf16[2,2,192,768]{3,1,0,2:T(2,128)(2,1)}), bf16[2,2,192,768]{3,1,0,2:T(2,128)(2,1)}, u32[]{:S(2)}, u32[]{:S(2)}) %all-to-all-start.2) | async-done | bytes 1179680 | tf_op jit(solution)/shard_map/all_to_all | solution.py:279
  392.3 8.3 %fusion.13 = (f32[2,24,12,16]{3,2,1,0:T(8,128)S(1)}, bf16[2,24,12,16,16]{3,4,2,1,0:T(8,128)(2,1)S(1)}) fusion(f32[2,24,12,16,16]{3,4,2,1,0:T(8,128)} %copy-done.3, f32[2,24,12,16]{3,2,1,0:T(8,128)S(1)} %log_add_fusion, bf16[2,16,24,1,12,64]{5,4,3,2,1,0:T(8,128)(2,1)} %copy-done.15, bf16[2,16,24,12,64]{4,3,2,1,0:T(8,128)(2,1)} %reshape.349), kind=kOutput, calls=%fused_computation.46 | convolution fusion | flops 19749888 | bytes 3317760 | tf_op jit(solution)/shard_map/blghd,bmghd->bghlm/dot_general | solution.py:98
  412.4 9.1 %copy.190 = bf16[2,16,24,3,12,64]{5,4,3,2,1,0:T(8,128)(2,1)} copy(bf16[2,16,24,3,12,64]{5,1,4,2,0,3:T(8,128)(2,1)} %maximum_convert_fusion) | data formatting | bytes 7077888 | tf_op jit(solution)/shard_map/convert_element_type | solution.py:132
  421.5 12.0 %convert_element_type.286 = bf16[768,2304]{1,0:T(8,128)(2,1)} reshape(bf16[2,16,24,3,12,64]{5,4,3,2,1,0:T(8,128)(2,1)} %copy.190) | data formatting | bytes 7077888 | tf_op jit(solution)/shard_map/convert_element_type | solution.py:132
  433.5 12.2 %convert_element_type.289 = bf16[2,16,24,2304]{3,2,1,0:T(8,128)(2,1)} reshape(bf16[2,16,24,3,12,64]{5,4,3,2,1,0:T(8,128)(2,1)} %copy.190) | data formatting | bytes 7077888 | tf_op jit(solution)/shard_map/convert_element_type | solution.py:132
  476.1 17.6 %all-to-all-done.3 = bf16[2,16,24,768]{3,2,0,1:T(8,128)(2,1)} async-done(((bf16[2,16,24,768]{3,2,0,1:T(8,128)(2,1)}), bf16[2,16,24,768]{3,2,0,1:T(8,128)(2,1)}, u32[]{:S(2)}, u32[]{:S(2)}) %all-to-all-start.3) | async-done | bytes 1179680 | tf_op jit(solution)/shard_map/all_to_all | solution.py:289
  509.7 9.5 %fusion.1 = (f32[4,12,192]{2,1,0:T(8,128)S(1)}, bf16[4,12,192,192]{2,3,1,0:T(8,128)(2,1)}) fusion(f32[4,12,192,192]{2,3,1,0:T(8,128)} %copy-done.2, f32[4,12,192]{2,1,0:T(8,128)S(1)} %copy-done.29, bf16[4,192,12,64]{1,3,2,0:T(8,128)(2,1)} %bitcast.275, bf16[4,192,3,12,64]{1,4,3,2,0:T(8,128)(2,1)} %bitcast.267), kind=kOutput, calls=%fused_computation.6 | convolution fusion | flops 237100032 | bytes 16195584 | tf_op jit(solution)/shard_map/glhd,gmhd->ghlm/dot_general | solution.py:98
  519.2 10.1 %fusion.3 = bf16[4,12,192,192]{2,3,1,0:T(8,128)(2,1)} fusion(bf16[4,12,192,192]{2,3,1,0:T(8,128)(2,1)} %get-tuple-element.114, f32[4,12,192,192]{2,3,1,0:T(8,128)} %copy-done.2, f32[4,12,192]{2,1,0:T(8,128)S(1)} %get-tuple-element.113, f32[4,12,192]{2,1,0:T(8,128)S(1)} %copy-done.29), kind=kLoop, calls=%fused_computation.8 | loop fusion | flops 10616832 | bytes 14229504 | tf_op jit(solution)/shard_map/convert_element_type | solution.py:106
  550.2 8.9 %convert_element_type.308 = bf16[768,2304]{0,1:T(8,128)(2,1)} reshape(bf16[4,192,3,12,64]{1,0,4,3,2:T(4,128)(2,1)} %copy.202) | data formatting | bytes 7077888 | tf_op jit(solution)/shard_map/convert_element_type | solution.py:132
  559.2 6.9 fusion.48
  577.3 9.0 %add_bitcast_fusion = f32[2,1,2,192,768]{4,3,2,1,0:T(8,128)} fusion(f32[2,2,192,768]{3,2,1,0:T(8,128)S(1)} %get-tuple-element.109, bf16[2,2,192,3072]{3,2,1,0:T(8,128)(2,1)} %multiply_convert_fusion, bf16[3072,768,1,1]{1,0,3,2:T(8,128)(2,1)} %bitcast.281), kind=kOutput, calls=%fused_computation.107 | convolution fusion | flops 3624468480 | bytes 14155776 | tf_op jit(solution)/shard_map/dot_general | solution.py:34
  602.1 49.5 %reduce-scatter.4.cloned.1.call-done = bf16[48,3200]{1,0:T(8,128)(2,1)} async-done(((bf16[768,3200]{1,0:T(8,128)(2,1)}), bf16[48,3200]{1,0:T(8,128)(2,1)}) %reduce-scatter.4.cloned.1.call-update) | async-done | bytes 307216 | tf_op jit(solution)/shard_map/reduce_scatter | solution.py:214
  661.3 104.3 %reduce-scatter.8.cloned.1.call-done = bf16[48,6144]{1,0:T(8,128)(2,1)} async-done(((bf16[768,6144]{1,0:T(8,128)(2,1)}), bf16[48,6144]{1,0:T(8,128)(2,1)}) %reduce-scatter.8.cloned.1.call-update) | async-done | bytes 589840 | tf_op jit(solution)/shard_map/reduce_scatter | solution.py:214
  767.2 13.5 %collective-permute-done.4 = bf16[48,6144]{1,0:T(8,128)(2,1)S(1)} collective-permute-done((bf16[48,6144]{1,0:T(8,128)(2,1)}, bf16[48,6144]{1,0:T(8,128)(2,1)S(1)}, u32[]{:S(2)}, u32[]{:S(2)}) %collective-permute-start.4) | collective-permute-done | bytes 589856 | tf_op jit(solution)/shard_map/ppermute | solution.py:192
  (290 shorter events, 250.1 us)
Async XLA Ops:
  7.2 60.5 %all-gather.3.cloned.1.call-start = ((), (), s32[]{:S(2)}) async-start(), calls=%async_computation.7 | async-start | bytes 5222400 | tf_op jit(solution)/shard_map/all_gather | solution.py:186
  10.7 184.0 %all-gather.5.cloned.1.call-start = ((), (), s32[]{:S(2)}) async-start(), calls=%async_computation.8 | async-start | bytes 15040512 | tf_op jit(solution)/shard_map/all_gather | solution.py:186
  19.6 57.2 %copy-start.53 = (f32[4,192]{1,0:T(4,128)}, f32[4,192]{1,0:T(4,128)S(1)}, u32[]{:S(2)}) copy-start(f32[4,192]{1,0:T(4,128)S(1)} %rsqrt.37) | copy-start | bytes 9220
  69.3 28.0 %copy-start.45 = (f32[768]{0:T(1024)}, f32[768]{0:T(1024)S(1)}, u32[]{:S(2)}) copy-start(f32[768]{0:T(1024)S(1)} %get-tuple-element.71) | copy-start | bytes 9220
  97.3 60.5 %copy-start.49 = (f32[2,2,192]{2,1,0:T(2,128)}, f32[2,2,192]{2,1,0:T(2,128)S(1)}, u32[]{:S(2)}) copy-start(f32[2,2,192]{2,1,0:T(2,128)S(1)} %multiply_reduce_fusion.4) | copy-start | bytes 9220
  97.3 60.4 %copy-start.43 = (f32[2,2,192]{2,1,0:T(2,128)}, f32[2,2,192]{2,1,0:T(2,128)S(1)}, u32[]{:S(2)}) copy-start(f32[2,2,192]{2,1,0:T(2,128)S(1)} %fusion.70) | copy-start | bytes 9220
  157.9 43.2 %copy-start.33 = (bf16[2,8,2,24,768]{4,3,2,1,0:T(8,128)(2,1)}, bf16[2,8,2,24,768]{4,3,2,1,0:T(8,128)(2,1)S(1)}, u32[]{:S(2)}) copy-start(bf16[2,8,2,24,768]{4,3,2,1,0:T(8,128)(2,1)S(1)} %copy.174) | copy-start | bytes 3538948
  232.4 32.9 %all-to-all-start.1 = ((bf16[2,16,24,768]{3,2,0,1:T(8,128)(2,1)}), bf16[2,16,24,768]{3,2,0,1:T(8,128)(2,1)S(1)}, u32[]{:S(2)}, u32[]{:S(2)}) async-start(bf16[2,16,24,768]{3,2,0,1:T(8,128)(2,1)} %reshape.368), calls=%async_computation.1 | async-start | bytes 2359296 | tf_op jit(solution)/shard_map/all_to_all | solution.py:253
  279.5 26.4 %copy-start.9 = (f32[2,2,192,3072]{3,2,1,0:T(8,128)}, f32[2,2,192,3072]{3,2,1,0:T(8,128)S(1)}, u32[]{:S(2)}) copy-start(f32[2,2,192,3072]{3,2,1,0:T(8,128)S(1)} %get-tuple-element.110) | copy-start | bytes 28311556
  352.0 33.1 %all-to-all-start.2 = ((bf16[2,2,192,768]{3,1,0,2:T(2,128)(2,1)}), bf16[2,2,192,768]{3,1,0,2:T(2,128)(2,1)}, u32[]{:S(2)}, u32[]{:S(2)}) async-start(bf16[2,2,192,768]{3,1,0,2:T(2,128)(2,1)} %copy.185), calls=%async_computation.2 | async-start | bytes 2359296 | tf_op jit(solution)/shard_map/all_to_all | solution.py:279
  387.6 13.0 %slice-start.3 = ((s8[4718592]{0:T(1024)(128)(4,1)}), s8[524288]{0:T(1024)(128)(4,1)S(1)}, s32[]{:S(2)}) async-start(s8[4718592]{0:T(1024)(128)(4,1)} %bitcast.263), calls=%async_computation.15 | async-start | bytes 1048576
  461.1 32.6 %all-to-all-start.3 = ((bf16[2,16,24,768]{3,2,0,1:T(8,128)(2,1)}), bf16[2,16,24,768]{3,2,0,1:T(8,128)(2,1)}, u32[]{:S(2)}, u32[]{:S(2)}) async-start(bf16[2,16,24,768]{3,2,0,1:T(8,128)(2,1)} %copy.194), calls=%async_computation.3 | async-start | bytes 2359296 | tf_op jit(solution)/shard_map/all_to_all | solution.py:289
  465.4 124.5 %reduce-scatter.6.cloned.1.call-start = ((), (), s32[]{:S(2)}) async-start(), calls=%async_computation.10 | async-start | bytes 5013504 | tf_op jit(solution)/shard_map/reduce_scatter | solution.py:214
  476.0 19.2 %copy-start.46 = (f32[768]{0:T(1024)S(1)}, f32[768]{0:T(1024)}, u32[]{:S(2)}) copy-start(f32[768]{0:T(1024)} %copy-done.45) | copy-start | bytes 9220
  476.0 175.6 %reduce-scatter.4.cloned.1.call-start = ((), (), s32[]{:S(2)}) async-start(), calls=%async_computation.9 | async-start | bytes 5222400 | tf_op jit(solution)/shard_map/reduce_scatter | solution.py:214
  519.2 18.7 %slice-start = ((s8[9437184]{0:T(1024)(128)(4,1)}), s8[4194304]{0:T(1024)(128)(4,1)S(1)}, s32[]{:S(2)}) async-start(s8[9437184]{0:T(1024)(128)(4,1)} %bitcast.261), calls=%async_computation.12 | async-start | bytes 8388608
  519.2 18.7 %slice-start.1 = ((s8[9437184]{0:T(1024)(128)(4,1)}), s8[1048576]{0:T(1024)(128)(4,1)S(1)}, s32[]{:S(2)}) async-start(s8[9437184]{0:T(1024)(128)(4,1)} %bitcast.261), calls=%async_computation.13 | async-start | bytes 2097152
  576.7 189.0 %reduce-scatter.8.cloned.1.call-start = ((), (), s32[]{:S(2)}) async-start(), calls=%async_computation.11 | async-start | bytes 10027008 | tf_op jit(solution)/shard_map/reduce_scatter | solution.py:214
  589.9 7.3 collective-permute-start.2
  598.2 54.8 %collective-permute-start.3 = (bf16[48,3072]{1,0:T(8,128)(2,1)S(1)}, bf16[48,3072]{1,0:T(8,128)(2,1)S(1)}, u32[]{:S(2)}, u32[]{:S(2)}) collective-permute-start(bf16[48,3072]{1,0:T(8,128)(2,1)S(1)} %add.117), channel_id=1, source_target_pairs={{0,8},{8,0},{1,9},{9,1},{2,10},{10,2},{3,11},{11,3},{4,12},{12,4},... | collective-permute-start | bytes 884744 | tf_op jit(solution)/shard_map/ppermute | solution.py:198
  651.6 7.5 collective-permute-start
  660.3 106.8 %collective-permute-start.1 = (bf16[48,3200]{1,0:T(8,128)(2,1)S(1)}, bf16[48,3200]{1,0:T(8,128)(2,1)S(1)}, u32[]{:S(2)}, u32[]{:S(2)}) collective-permute-start(bf16[48,3200]{1,0:T(8,128)(2,1)S(1)} %add.116), channel_id=1, source_target_pairs={{0,8},{8,0},{1,9},{9,1},{2,10},{10,2},{3,11},{11,3},{4,12},{12,4},... | collective-permute-start | bytes 921608 | tf_op jit(solution)/shard_map/ppermute | solution.py:198
  765.7 15.0 %collective-permute-start.4 = (bf16[48,6144]{1,0:T(8,128)(2,1)}, bf16[48,6144]{1,0:T(8,128)(2,1)S(1)}, u32[]{:S(2)}, u32[]{:S(2)}) collective-permute-start(bf16[48,6144]{1,0:T(8,128)(2,1)} %reduce-scatter.8.cloned.1.call-done), channel_id=1, source_target_pairs={{0,16},{16,0},{1,17},{17,1},{2,18},{18,2},{3,19},{19,3},{4,20},{20... | collective-permute-start | bytes 1769480 | tf_op jit(solution)/shard_map/ppermute | solution.py:192
  781.8 2.5 collective-permute-start.5
  (57 other events, 245.1 us)
Sparse Core Ops, SparseCore 0:
  10.9 56.8 all-gather.2
  70.6 124.1 all-gather.4
  476.2 76.9 reduce-scatter.5
  576.8 74.7 reduce-scatter.3
  655.5 110.0 reduce-scatter.7

commit v3 on v2

--- a/solution.py
+++ b/solution.py
@@ -228,12 +228,8 @@
     s_in, s_out, gains = gather_group(
         (space_in, space_out, norm_gains), ("plain", "plain", "gains"), core, half
     )
-    t_in, t_out, h_in, h_out = gather_group(
-        (time_in, time_out, hidden_in, hidden_out),
-        ("plain", "plain", "plain", "grouped"),
-        core,
-        half,
-    )
+    t_in, t_out = gather_group((time_in, time_out), ("plain", "plain"), core, half)
+    h_in, h_out = gather_group((hidden_in, hidden_out), ("plain", "grouped"), core, half)
     gain_rows = gains.astype(jnp.float32)
 
     micro, _, frames, places, _ = inputs.shape

time: 800 us -> 787 us (0.984)
  waiting for transfers between devices: 322 us -> 271 us
  blocking collectives: 57.9 us -> 104 us
    all_to_all x0 -> x1, blocking collectives: none -> 60 us  [layer(): lax.all_to_all(context_placed, 'fsdp', split_axis=1, concat_axis=2, tiled...]
    all_gather x2 -> x3, waiting for transfers between devices: 83.2 us -> 50.1 us  [gather_group(): gathered = lax.all_gather(block, MEMBERS, axis=0, tiled=True)]
    all_to_all x1 -> x0, waiting for transfers between devices: 17.7 us -> none  [layer(): lax.all_to_all(context_placed, 'fsdp', split_axis=1, concat_axis=2, tiled...]
    all_to_all x1, blocking collectives: 57.9 us -> 43.9 us  [layer(): lax.all_to_all(normed_two, 'fsdp', split_axis=2, concat_axis=1, tiled=True)]
    unnamed x140 -> x136, local copies, waits for them, and re-layouts: 20.3 us -> 13.6 us
  transfers between devices with their start and end apart: 14 -> 14, of which waited for: 10 -> 8; matrix products, arithmetic and copies ran while one was open for 20% -> 25% of each run, Pallas kernels for 0% -> 0%
where the time goes in v3:
time: 787 us; the launch traced here: 781 us
  waiting for transfers between devices  271 us (34%)
  matrix products  147 us (19%)
  local copies, waits for them, and re-layouts  126 us (16%)
  other arithmetic  104 us (13%)
  blocking collectives  104 us (13%)
  between operations  15.6 us (2%)
  starting transfers between devices  14.3 us (2%)
    reduce_scatter x3, waiting for transfers between devices, reduce_group(): owned = lax.psum_scatter(packed, MEMBERS, scatter_dimension=0, tiled=True)  154 us
    all_to_all x1, blocking collectives, layer(): lax.all_to_all(context_placed, 'fsdp', split_axis=1, concat_axis=2, tiled...  60 us
    convert_element_type x6, local copies, waits for them, and re-layouts, attend_back(): stacked.reshape(back_context.shape[:-1] + (3 * D,)).astype(jnp.bfloat16)  51.4 us
    all_gather x3, waiting for transfers between devices, gather_group(): gathered = lax.all_gather(block, MEMBERS, axis=0, tiled=True)  50.1 us
    all_to_all x1, blocking collectives, layer(): lax.all_to_all(normed_two, 'fsdp', split_axis=2, concat_axis=1, tiled=True)  43.9 us
    dot_general x6, matrix products, flat_dot(): product = jnp.dot(flat, right, preferred_element_type=jnp.float32)  39.4 us
    dot_general x6, matrix products, back_dot(): lax.dot_general(flat, right, (((1,), (1,)), ((), ())), preferred_element_...  32.7 us
    dot_general x6, matrix products, token_sum(): lax.dot_general(left_rows, right_rows, (((0,), (0,)), ((), ())), preferre...  28.3 us
  transfers between devices with their start and end apart: 14, of which 8 were waited for; matrix products, arithmetic and copies ran while one was open for 25% of the time, Pallas kernels for 0%

profile of v3, /device:TPU:0, one launch (start us, length us, event | category | flops | bytes accessed | tf_op | source)
XLA Modules:
  0.0 780.9 jit_solution(3664700016322363873)
XLA Ops:
  17.6 50.1 %all-gather.4.cloned.1.call-done = bf16[768,3200]{1,0:T(8,128)(2,1)} async-done(((bf16[48,3200]{1,0:T(8,128)(2,1)}), bf16[768,3200]{1,0:T(8,128)(2,1)}) %all-gather.4.cloned.1.call-update) | async-done | bytes 4915216 | tf_op jit(solution)/shard_map/all_gather | solution.py:186
  69.3 7.5 convolution_convert_fusion.3
  99.9 43.9 %all_to_all.54 = bf16[2,2,192,768]{3,1,0,2:T(2,128)(2,1)S(1)} all-to-all(bf16[2,2,192,768]{3,1,0,2:T(2,128)(2,1)S(1)} %copy.172), channel_id=1, replica_groups=mesh['dpo'=2,'core'=2,'fsdp'=8] {'fsdp'}, dimensions={2} | all-to-all | bytes 2359296 | tf_op jit(solution)/shard_map/all_to_all | solution.py:247
  144.0 6.8 convolution_convert_fusion.2
  150.8 11.6 %reshape.341 = bf16[2,16,24,3,12,64]{5,4,3,2,1,0:T(8,128)(2,1)} reshape(bf16[2,16,24,2304]{3,2,1,0:T(8,128)(2,1)} %convolution_convert_fusion.2) | data formatting | bytes 7077888 | tf_op jit(solution)/shard_map/reshape | solution.py:55
  181.3 60.0 %all_to_all.55 = bf16[2,16,24,768]{3,2,0,1:T(8,128)(2,1)S(1)} all-to-all(bf16[2,16,24,768]{3,2,0,1:T(8,128)(2,1)S(1)} %reshape.368), channel_id=1, replica_groups=mesh['dpo'=2,'core'=2,'fsdp'=8] {'fsdp'}, dimensions={1} | all-to-all | bytes 2359296 | tf_op jit(solution)/shard_map/all_to_all | solution.py:249
  255.1 10.0 %fusion.42 = (u8[2,192,3072]{2,1,0:T(8,128)(4,1)S(1)}, u8[2,192,3072]{2,1,0:T(8,128)(4,1)}, f32[2,2,192,3072]{3,2,1,0:T(8,128)S(1)}) fusion(bf16[768,6144]{1,0:T(8,128)(2,1)} %all-gather.8.cloned.1.call-done, f32[2,2,192,768]{3,2,1,0:T(8,128)S(1)} %get-tuple-element.109, f32[768]{0:T(1024)S(1)} %get-tuple-element.70, f32[2,2,192]{2,1,0:T(2,128)S(1)} %fusion.71, ...), kind=kOutput, calls=%fused_computation.115 | convolution fusion | flops 3654549504 | bytes 18883584 | tf_op jit(solution)/shard_map/dot_general | solution.py:34
  265.1 26.3 %add_convert_fusion = (bf16[2,2,192,3072]{3,2,1,0:T(8,128)(2,1)S(1)}, f32[2,2,192,3072]{3,2,1,0:T(8,128)}) fusion(f32[2,2,192,3072]{3,2,1,0:T(8,128)} %bitcast.275, f32[2,2,192,3072]{3,2,1,0:T(8,128)S(1)} %get-tuple-element.110, u8[2,192,3072]{2,1,0:T(8,128)(4,1)} %get-tuple-element.63, u8[2,192,3072]{2,1,0:T(8,128)(4,1)S(1)} %get-tuple-element.62), kind=kLoop, calls=%fused_computation.18 | loop fusion | flops 181665792 | bytes 35389440 | tf_op jit(solution)/shard_map/convert_element_type | solution.py:261
  297.8 10.9 %multiply_convert_fusion = bf16[2,2,192,3072]{3,2,1,0:T(8,128)(2,1)} fusion(f32[2,2,192,3072]{3,2,1,0:T(8,128)} %get-tuple-element.76, f32[2,2,192,3072]{3,2,1,0:T(8,128)} %copy-done.10), kind=kLoop, calls=%fused_computation.19 | loop fusion | flops 7077888 | bytes 23592960 | tf_op jit(solution)/shard_map/convert_element_type | solution.py:253
  322.3 7.6 fusion.49
  347.1 24.8 %all-to-all-done.2 = bf16[2,2,192,768]{3,1,0,2:T(2,128)(2,1)} async-done(((bf16[2,2,192,768]{3,1,0,2:T(2,128)(2,1)}), bf16[2,2,192,768]{3,1,0,2:T(2,128)(2,1)}, u32[]{:S(2)}, u32[]{:S(2)}) %all-to-all-start.2) | async-done | bytes 1179680 | tf_op jit(solution)/shard_map/all_to_all | solution.py:275
  379.1 8.3 %fusion.13 = (f32[2,24,12,16]{3,2,1,0:T(8,128)S(1)}, bf16[2,24,12,16,16]{3,4,2,1,0:T(8,128)(2,1)S(1)}) fusion(f32[2,24,12,16,16]{3,4,2,1,0:T(8,128)} %copy-done.3, f32[2,24,12,16]{3,2,1,0:T(8,128)S(1)} %log_add_fusion, bf16[2,16,24,1,12,64]{5,4,3,2,1,0:T(8,128)(2,1)} %copy-done.16, bf16[2,16,24,12,64]{4,3,2,1,0:T(8,128)(2,1)} %reshape.349), kind=kOutput, calls=%fused_computation.46 | convolution fusion | flops 19749888 | bytes 3317760 | tf_op jit(solution)/shard_map/blghd,bmghd->bghlm/dot_general | solution.py:98
  399.3 9.2 %copy.190 = bf16[2,16,24,3,12,64]{5,4,3,2,1,0:T(8,128)(2,1)} copy(bf16[2,16,24,3,12,64]{5,1,4,2,0,3:T(8,128)(2,1)} %maximum_convert_fusion) | data formatting | bytes 7077888 | tf_op jit(solution)/shard_map/convert_element_type | solution.py:132
  408.4 12.0 %convert_element_type.286 = bf16[768,2304]{1,0:T(8,128)(2,1)} reshape(bf16[2,16,24,3,12,64]{5,4,3,2,1,0:T(8,128)(2,1)} %copy.190) | data formatting | bytes 7077888 | tf_op jit(solution)/shard_map/convert_element_type | solution.py:132
  420.4 12.2 %convert_element_type.289 = bf16[2,16,24,2304]{3,2,1,0:T(8,128)(2,1)} reshape(bf16[2,16,24,3,12,64]{5,4,3,2,1,0:T(8,128)(2,1)} %copy.190) | data formatting | bytes 7077888 | tf_op jit(solution)/shard_map/convert_element_type | solution.py:132
  463.0 17.6 %all-to-all-done.3 = bf16[2,16,24,768]{3,2,0,1:T(8,128)(2,1)} async-done(((bf16[2,16,24,768]{3,2,0,1:T(8,128)(2,1)}), bf16[2,16,24,768]{3,2,0,1:T(8,128)(2,1)}, u32[]{:S(2)}, u32[]{:S(2)}) %all-to-all-start.3) | async-done | bytes 1179680 | tf_op jit(solution)/shard_map/all_to_all | solution.py:285
  496.6 9.5 %fusion.1 = (f32[4,12,192]{2,1,0:T(8,128)S(1)}, bf16[4,12,192,192]{2,3,1,0:T(8,128)(2,1)}) fusion(f32[4,12,192,192]{2,3,1,0:T(8,128)} %copy-done.2, f32[4,12,192]{2,1,0:T(8,128)S(1)} %copy-done.30, bf16[4,192,12,64]{1,3,2,0:T(8,128)(2,1)} %bitcast.273, bf16[4,192,3,12,64]{1,4,3,2,0:T(8,128)(2,1)} %bitcast.267), kind=kOutput, calls=%fused_computation.6 | convolution fusion | flops 237100032 | bytes 16195584 | tf_op jit(solution)/shard_map/glhd,gmhd->ghlm/dot_general | solution.py:98
  506.1 10.2 %fusion.3 = bf16[4,12,192,192]{2,3,1,0:T(8,128)(2,1)} fusion(bf16[4,12,192,192]{2,3,1,0:T(8,128)(2,1)} %get-tuple-element.114, f32[4,12,192,192]{2,3,1,0:T(8,128)} %copy-done.2, f32[4,12,192]{2,1,0:T(8,128)S(1)} %get-tuple-element.113, f32[4,12,192]{2,1,0:T(8,128)S(1)} %copy-done.30), kind=kLoop, calls=%fused_computation.8 | loop fusion | flops 10616832 | bytes 14229504 | tf_op jit(solution)/shard_map/convert_element_type | solution.py:106
  537.3 9.0 %convert_element_type.308 = bf16[768,2304]{0,1:T(8,128)(2,1)} reshape(bf16[4,192,3,12,64]{1,0,4,3,2:T(4,128)(2,1)} %copy.202) | data formatting | bytes 7077888 | tf_op jit(solution)/shard_map/convert_element_type | solution.py:132
  546.2 6.9 fusion.48
  564.4 9.0 %add_bitcast_fusion = f32[2,1,2,192,768]{4,3,2,1,0:T(8,128)} fusion(f32[2,2,192,768]{3,2,1,0:T(8,128)S(1)} %get-tuple-element.109, bf16[2,2,192,3072]{3,2,1,0:T(8,128)(2,1)} %multiply_convert_fusion, bf16[3072,768,1,1]{1,0,3,2:T(8,128)(2,1)} %bitcast.279), kind=kOutput, calls=%fused_computation.107 | convolution fusion | flops 3624468480 | bytes 14155776 | tf_op jit(solution)/shard_map/dot_general | solution.py:34
  589.2 49.5 %reduce-scatter.4.cloned.1.call-done = bf16[48,3200]{1,0:T(8,128)(2,1)} async-done(((bf16[768,3200]{1,0:T(8,128)(2,1)}), bf16[48,3200]{1,0:T(8,128)(2,1)}) %reduce-scatter.4.cloned.1.call-update) | async-done | bytes 307216 | tf_op jit(solution)/shard_map/reduce_scatter | solution.py:214
  648.6 104.1 %reduce-scatter.8.cloned.1.call-done = bf16[48,6144]{1,0:T(8,128)(2,1)} async-done(((bf16[768,6144]{1,0:T(8,128)(2,1)}), bf16[48,6144]{1,0:T(8,128)(2,1)}) %reduce-scatter.8.cloned.1.call-update) | async-done | bytes 589840 | tf_op jit(solution)/shard_map/reduce_scatter | solution.py:214
  754.3 13.4 %collective-permute-done.4 = bf16[48,6144]{1,0:T(8,128)(2,1)S(1)} collective-permute-done((bf16[48,6144]{1,0:T(8,128)(2,1)}, bf16[48,6144]{1,0:T(8,128)(2,1)S(1)}, u32[]{:S(2)}, u32[]{:S(2)}) %collective-permute-start.4) | collective-permute-done | bytes 589856 | tf_op jit(solution)/shard_map/ppermute | solution.py:192
  (290 shorter events, 235.1 us)
Async XLA Ops:
  7.2 60.5 %all-gather.4.cloned.1.call-start = ((), (), s32[]{:S(2)}) async-start(), calls=%async_computation.7 | async-start | bytes 5222400 | tf_op jit(solution)/shard_map/all_gather | solution.py:186
  10.7 133.3 %all-gather.6.cloned.1.call-start = ((), (), s32[]{:S(2)}) async-start(), calls=%async_computation.8 | async-start | bytes 5013504 | tf_op jit(solution)/shard_map/all_gather | solution.py:186
  13.4 231.4 %all-gather.8.cloned.1.call-start = ((), (), s32[]{:S(2)}) async-start(), calls=%async_computation.9 | async-start | bytes 10027008 | tf_op jit(solution)/shard_map/all_gather | solution.py:186
  15.9 61.0 %copy-start.56 = (f32[4,192]{1,0:T(4,128)}, f32[4,192]{1,0:T(4,128)S(1)}, u32[]{:S(2)}) copy-start(f32[4,192]{1,0:T(4,128)S(1)} %rsqrt.37) | copy-start | bytes 9220
  69.3 28.1 %copy-start.48 = (f32[768]{0:T(1024)}, f32[768]{0:T(1024)S(1)}, u32[]{:S(2)}) copy-start(f32[768]{0:T(1024)S(1)} %get-tuple-element.71) | copy-start | bytes 9220
  97.4 46.4 %copy-start.52 = (f32[2,2,192]{2,1,0:T(2,128)}, f32[2,2,192]{2,1,0:T(2,128)S(1)}, u32[]{:S(2)}) copy-start(f32[2,2,192]{2,1,0:T(2,128)S(1)} %multiply_reduce_fusion.4) | copy-start | bytes 9220
  97.4 46.4 %copy-start.46 = (f32[2,2,192]{2,1,0:T(2,128)}, f32[2,2,192]{2,1,0:T(2,128)S(1)}, u32[]{:S(2)}) copy-start(f32[2,2,192]{2,1,0:T(2,128)S(1)} %fusion.70) | copy-start | bytes 9220
  181.3 60.1 %copy-start.5 = (f32[2,2,192,768]{3,2,1,0:T(8,128)S(1)}, f32[2,2,192,768]{3,2,1,0:T(8,128)}, u32[]{:S(2)}) copy-start(f32[2,2,192,768]{3,2,1,0:T(8,128)} %copy-done.4) | copy-start | bytes 7077892
  265.1 26.3 %copy-start.10 = (f32[2,2,192,3072]{3,2,1,0:T(8,128)}, f32[2,2,192,3072]{3,2,1,0:T(8,128)S(1)}, u32[]{:S(2)}) copy-start(f32[2,2,192,3072]{3,2,1,0:T(8,128)S(1)} %get-tuple-element.110) | copy-start | bytes 28311556
  338.6 33.3 %all-to-all-start.2 = ((bf16[2,2,192,768]{3,1,0,2:T(2,128)(2,1)}), bf16[2,2,192,768]{3,1,0,2:T(2,128)(2,1)}, u32[]{:S(2)}, u32[]{:S(2)}) async-start(bf16[2,2,192,768]{3,1,0,2:T(2,128)(2,1)} %copy.185), calls=%async_computation.2 | async-start | bytes 2359296 | tf_op jit(solution)/shard_map/all_to_all | solution.py:275
  374.3 13.1 %slice-start.3 = ((s8[4718592]{0:T(1024)(128)(4,1)}), s8[524288]{0:T(1024)(128)(4,1)S(1)}, s32[]{:S(2)}) async-start(s8[4718592]{0:T(1024)(128)(4,1)} %bitcast.263), calls=%async_computation.16 | async-start | bytes 1048576
  448.0 32.6 %all-to-all-start.3 = ((bf16[2,16,24,768]{3,2,0,1:T(8,128)(2,1)}), bf16[2,16,24,768]{3,2,0,1:T(8,128)(2,1)}, u32[]{:S(2)}, u32[]{:S(2)}) async-start(bf16[2,16,24,768]{3,2,0,1:T(8,128)(2,1)} %copy.194), calls=%async_computation.3 | async-start | bytes 2359296 | tf_op jit(solution)/shard_map/all_to_all | solution.py:285
  452.3 124.6 %reduce-scatter.6.cloned.1.call-start = ((), (), s32[]{:S(2)}) async-start(), calls=%async_computation.11 | async-start | bytes 5013504 | tf_op jit(solution)/shard_map/reduce_scatter | solution.py:214
  462.9 19.2 %copy-start.49 = (f32[768]{0:T(1024)S(1)}, f32[768]{0:T(1024)}, u32[]{:S(2)}) copy-start(f32[768]{0:T(1024)} %copy-done.48) | copy-start | bytes 9220
  462.9 175.7 %reduce-scatter.4.cloned.1.call-start = ((), (), s32[]{:S(2)}) async-start(), calls=%async_computation.10 | async-start | bytes 5222400 | tf_op jit(solution)/shard_map/reduce_scatter | solution.py:214
  506.1 18.7 %slice-start = ((s8[9437184]{0:T(1024)(128)(4,1)}), s8[4194304]{0:T(1024)(128)(4,1)S(1)}, s32[]{:S(2)}) async-start(s8[9437184]{0:T(1024)(128)(4,1)} %bitcast.261), calls=%async_computation.13 | async-start | bytes 8388608
  506.1 18.7 %slice-start.1 = ((s8[9437184]{0:T(1024)(128)(4,1)}), s8[1048576]{0:T(1024)(128)(4,1)S(1)}, s32[]{:S(2)}) async-start(s8[9437184]{0:T(1024)(128)(4,1)} %bitcast.261), calls=%async_computation.14 | async-start | bytes 2097152
  563.8 188.9 %reduce-scatter.8.cloned.1.call-start = ((), (), s32[]{:S(2)}) async-start(), calls=%async_computation.12 | async-start | bytes 10027008 | tf_op jit(solution)/shard_map/reduce_scatter | solution.py:214
  577.0 7.3 collective-permute-start.2
  585.3 54.8 %collective-permute-start.3 = (bf16[48,3072]{1,0:T(8,128)(2,1)S(1)}, bf16[48,3072]{1,0:T(8,128)(2,1)S(1)}, u32[]{:S(2)}, u32[]{:S(2)}) collective-permute-start(bf16[48,3072]{1,0:T(8,128)(2,1)S(1)} %add.117), channel_id=1, source_target_pairs={{0,8},{8,0},{1,9},{9,1},{2,10},{10,2},{3,11},{11,3},{4,12},{12,4},... | collective-permute-start | bytes 884744 | tf_op jit(solution)/shard_map/ppermute | solution.py:198
  638.6 7.9 %collective-permute-start = (bf16[48,3200]{1,0:T(8,128)(2,1)}, bf16[48,3200]{1,0:T(8,128)(2,1)S(1)}, u32[]{:S(2)}, u32[]{:S(2)}) collective-permute-start(bf16[48,3200]{1,0:T(8,128)(2,1)} %reduce-scatter.4.cloned.1.call-done), channel_id=1, source_target_pairs={{0,16},{16,0},{1,17},{17,1},{2,18},{18,2},{3,19},{19,3},{4,20},{20... | collective-permute-start | bytes 921608 | tf_op jit(solution)/shard_map/ppermute | solution.py:192
  647.6 106.6 %collective-permute-start.1 = (bf16[48,3200]{1,0:T(8,128)(2,1)S(1)}, bf16[48,3200]{1,0:T(8,128)(2,1)S(1)}, u32[]{:S(2)}, u32[]{:S(2)}) collective-permute-start(bf16[48,3200]{1,0:T(8,128)(2,1)S(1)} %add.116), channel_id=1, source_target_pairs={{0,8},{8,0},{1,9},{9,1},{2,10},{10,2},{3,11},{11,3},{4,12},{12,4},... | collective-permute-start | bytes 921608 | tf_op jit(solution)/shard_map/ppermute | solution.py:198
  752.7 15.0 %collective-permute-start.4 = (bf16[48,6144]{1,0:T(8,128)(2,1)}, bf16[48,6144]{1,0:T(8,128)(2,1)S(1)}, u32[]{:S(2)}, u32[]{:S(2)}) collective-permute-start(bf16[48,6144]{1,0:T(8,128)(2,1)} %reduce-scatter.8.cloned.1.call-done), channel_id=1, source_target_pairs={{0,16},{16,0},{1,17},{17,1},{2,18},{18,2},{3,19},{19,3},{4,20},{20... | collective-permute-start | bytes 1769480 | tf_op jit(solution)/shard_map/ppermute | solution.py:192
  768.9 2.5 collective-permute-start.5
  (56 other events, 223.9 us)
Sparse Core Ops, SparseCore 0:
  10.9 56.8 all-gather.3
  70.6 67.9 all-gather.5
  141.5 102.5 all-gather.7
  463.0 76.8 reduce-scatter.5
  563.9 74.7 reduce-scatter.3
  642.6 110.0 reduce-scatter.7
